TPU v7x, 32 devices: a whole 2x2x4 slice. The times are simulated.
32 devices in a mesh: tm: 4 (over y, x), space: 8 (over z, core).
Axes of the slice: x: 2, y: 2, z: 4, core: 2. Of those that a mesh axis runs over, the one named last changes fastest.
Arguments:
- residual: float32 [64, 64, 8, 128], P('tm', 'space'), may hold values from -24 to 24
- capacity: float32 [64, 8, 128], P('space'), may hold values from 0.25 to 4
Outputs:
- preconditioned: float32 [64, 64, 8, 128], P('tm', 'space')
All inputs are finite; a program needn't handle non-finite values.
Results may differ from a plain program's by a relative error of at most 0.0003.
Values sent between devices are 32-bit elements; how exact they have to be, the bound alone decides.
No kernel may reach another device: no remote copies, remote signals or barrier semaphores. Data moves between devices by JAX's collectives and lax.ppermute only.
A program may use at most 64 MiB of HBM per device.

v0:
```python
import functools
import math

import jax
import jax.numpy as jnp
from jax import lax
from jax.experimental import pallas as pl
from jax.experimental.pallas import tpu as pltpu
from jax.sharding import PartitionSpec as P

GRID_DEPTH = 4
SMOOTH = 2
COARSE_SWEEPS = 6


ALPHA_CORNER = 0.01
STEP_SIZE = 0.5
DIFFUSE = 2.0
ADVECT = (0.2, -0.15, 0.1)
OMEGA = 0.7
HIGHEST = lax.Precision.HIGHEST


def extended(array, sides, width):
    for axis, dim in sides:
        peers, length = (lax.axis_size(axis), array.shape[dim])
        up = [(i, (i + 1) % peers) for i in range(peers - 1)]
        down = [(j, i) for i, j in up]
        last = lax.slice_in_dim(array, length - width, length, axis=dim)
        initial = lax.slice_in_dim(array, 0, width, axis=dim)
        before = lax.ppermute(last, axis, up)
        after = lax.ppermute(initial, axis, down)
        array = jnp.concatenate([before, array, after], axis=dim)
    return array


def level_coefficients(per_level_values):
    spread = DIFFUSE / 4.0**per_level_values
    drifts = tuple((component / 2.0**per_level_values for component in ADVECT))
    return (spread, drifts)


def pad_second(volume, position):
    widths = [(0, 0)] * volume.ndim
    widths[position] = (1, 1)
    return jnp.pad(volume, widths)


def apply_operator(padded, current_capacity, spectral_shifts, per_level_values):
    spread, drifts = level_coefficients(per_level_values)
    centre = padded[:, :, 1:-1]
    upper_first = padded[:, :, 2:]
    lower_first = padded[:, :, :-2]
    wide_second = pad_second(centre, 3)
    upper_second = wide_second[:, :, :, 2:]
    lower_second = wide_second[:, :, :, :-2]
    wide_third = pad_second(centre, 4)
    upper_third = wide_third[:, :, :, :, 2:]
    lower_third = wide_third[:, :, :, :, :-2]
    stencil = spread * (
        6.0 * centre
        - upper_first
        - lower_first
        - upper_second
        - lower_second
        - upper_third
        - lower_third
    )
    stencil = (
        stencil
        + drifts[0] * (upper_first - lower_first)
        + drifts[1] * (upper_second - lower_second)
        + drifts[2] * (upper_third - lower_third)
    )
    first_shift, second_shift, third_shift = spectral_shifts
    real_part = centre[0]
    imag_part = centre[1]
    shifted = jnp.stack(
        [
            current_capacity * (first_shift * real_part - second_shift * imag_part),
            current_capacity * (second_shift * real_part + third_shift * imag_part),
        ]
    )
    return stencil + shifted


def inverse_diagonal(current_capacity, spectral_shifts, per_level_values):
    spread, drifts = level_coefficients(per_level_values)
    first_shift, second_shift, third_shift = spectral_shifts
    top_left = current_capacity * first_shift + 6.0 * spread
    coupling = current_capacity * second_shift
    bottom_right = current_capacity * third_shift + 6.0 * spread
    determinant = top_left * bottom_right + coupling * coupling
    return (bottom_right / determinant, coupling / determinant, top_left / determinant)


def damped_update(residual_now, inverse):
    diagonal_a, diagonal_b, diagonal_c = inverse
    return OMEGA * jnp.stack(
        [
            diagonal_a * residual_now[0] + diagonal_b * residual_now[1],
            diagonal_c * residual_now[1] - diagonal_b * residual_now[0],
        ]
    )


def restrict_to_coarse(volume):
    leading = volume.shape[:-3]
    first_extent, second_extent, third_extent = volume.shape[-3:]
    blocks = volume.reshape(
        leading + (first_extent // 2, 2, second_extent // 2, 2, third_extent // 2, 2)
    )
    lead_count = len(leading)
    return jnp.mean(blocks, axis=(lead_count + 1, lead_count + 3, lead_count + 5))


def prolong_cells(volume):
    leading = volume.shape[:-3]
    first_extent, second_extent, third_extent = volume.shape[-3:]
    expanded = jnp.broadcast_to(
        volume[..., :, None, :, None, :, None],
        leading + (first_extent, 2, second_extent, 2, third_extent, 2),
    )
    return expanded.reshape(leading + (2 * first_extent, 2 * second_extent, 2 * third_extent))


def shift_values(frequency, length):
    ratio_step = ALPHA_CORNER ** (1.0 / length)
    phases = 2.0 * math.pi / length * frequency.astype(jnp.float32)
    first_shift = (1.0 - ratio_step * jnp.cos(phases)) / STEP_SIZE
    second_shift = ratio_step * jnp.sin(phases) / STEP_SIZE
    leading = frequency == 0
    second_shift = jnp.where(leading, 0.0, second_shift)
    third_shift = jnp.where(leading, (1.0 + ratio_step) / STEP_SIZE, first_shift)
    return tuple(
        (column.reshape(-1, 1, 1, 1) for column in (first_shift, second_shift, third_shift))
    )


def phase_grid(row_count, length):
    integers = (
        jnp.arange(row_count, dtype=jnp.int32)[:, None]
        * jnp.arange(length, dtype=jnp.int32)[None, :]
        % length
    )
    return 2.0 * math.pi / length * integers.astype(jnp.float32)


def pad_faces(volume):
    return extended(volume, (("space", 2),), 1)


def multigrid_cycle(
    per_level_values,
    forcing_term,
    capacity_fields,
    spectral_shifts,
    shared_values,
    assemble_level,
    assemble_parts,
):
    current_capacity = capacity_fields[per_level_values]
    inverse = inverse_diagonal(current_capacity, spectral_shifts, per_level_values)
    coarsest = per_level_values == GRID_DEPTH - 1
    current = damped_update(forcing_term, inverse)
    for repeat in range((COARSE_SWEEPS if coarsest else SMOOTH) - 1):
        current = current + damped_update(
            forcing_term
            - apply_operator(
                pad_faces(current), current_capacity, spectral_shifts, per_level_values
            ),
            inverse,
        )
    if coarsest:
        return current
    coarse_right_hand = restrict_to_coarse(
        forcing_term
        - apply_operator(pad_faces(current), current_capacity, spectral_shifts, per_level_values)
    )
    coarse_solution = multigrid_cycle(
        per_level_values + 1,
        coarse_right_hand,
        capacity_fields,
        spectral_shifts,
        shared_values,
        assemble_level,
        assemble_parts,
    )
    current = current + prolong_cells(coarse_solution)
    for repeat in range(SMOOTH):
        current = current + damped_update(
            forcing_term
            - apply_operator(
                pad_faces(current), current_capacity, spectral_shifts, per_level_values
            ),
            inverse,
        )
    return current


def slab_program(residual, capacity):
    steps_here, thickness, extent_second, extent_third = residual.shape
    length = lax.axis_size("tm") * steps_here
    ratio_step = ALPHA_CORNER ** (1.0 / length)
    moments = (lax.axis_index("tm") * steps_here + jnp.arange(steps_here, dtype=jnp.int32)).astype(
        jnp.float32
    )
    scaled = (residual * jnp.power(ratio_step, moments)[:, None, None, None]).reshape(
        steps_here, -1
    )
    series = lax.all_to_all(scaled, "tm", split_axis=1, concat_axis=0, tiled=True)
    all_weights = jnp.power(ratio_step, jnp.arange(length, dtype=jnp.float32))
    alternate = 1.0 - 2.0 * (jnp.arange(length, dtype=jnp.int32) % 2).astype(jnp.float32)
    capacity_fields = [capacity]
    for per_level_values in range(1, GRID_DEPTH):
        capacity_fields.append(restrict_to_coarse(capacity_fields[-1]))
    halves = length // 2
    phases = phase_grid(halves, length)
    first_row = jnp.arange(halves, dtype=jnp.int32)[:, None] == 0
    forward = jnp.concatenate(
        [jnp.cos(phases), jnp.where(first_row, alternate[None, :], -jnp.sin(phases))], axis=0
    )
    spectrum = jnp.dot(forward, series, precision=HIGHEST).reshape(2, halves, -1)
    received = lax.all_to_all(spectrum, "tm", split_axis=1, concat_axis=2, tiled=True)
    slot_count = steps_here // 2
    frequency = lax.axis_index("tm") * slot_count + jnp.arange(slot_count, dtype=jnp.int32)
    spectral_shifts = shift_values(frequency, length)
    field_list = received.reshape(2, slot_count, thickness, extent_second, extent_third)
    solved_fields = multigrid_cycle(
        0, field_list, capacity_fields, spectral_shifts, False, GRID_DEPTH, None
    )
    flattened = solved_fields.reshape(2, slot_count, -1)
    returned = lax.all_to_all(flattened, "tm", split_axis=2, concat_axis=1, tiled=True)
    halves = length // 2
    phases = jnp.transpose(phase_grid(halves, length))
    first_column = jnp.arange(halves, dtype=jnp.int32)[None, :] == 0
    real_columns = jnp.where(first_column, 1.0, 2.0 * jnp.cos(phases)) / length
    imag_columns = jnp.where(first_column, alternate[:, None], -2.0 * jnp.sin(phases)) / length
    inverse_table = jnp.concatenate([real_columns, imag_columns], axis=1)
    values = jnp.dot(
        inverse_table,
        returned.reshape(returned.shape[0] * returned.shape[1], -1),
        precision=HIGHEST,
    )
    values = values / all_weights[:, None]
    result = lax.all_to_all(values, "tm", split_axis=0, concat_axis=1, tiled=True)
    return result.reshape(residual.shape)


def complex_add(p, q):
    return (p[0] + q[0], p[1] + q[1])


def complex_sub(p, q):
    return (p[0] - q[0], p[1] - q[1])


def complex_scale(p, cosine, sine):
    real, imag = p
    if abs(sine) < 1e-12:
        if abs(cosine - 1.0) < 1e-12:
            return p
        return (cosine * real, None if imag is None else cosine * imag)
    if imag is None:
        return (None if abs(cosine) < 1e-12 else cosine * real, sine * real)
    if abs(cosine) < 1e-12:
        if abs(sine - 1.0) < 1e-12:
            return (-imag, real)
        if abs(sine + 1.0) < 1e-12:
            return (imag, -real)
        return (-sine * imag, sine * real)
    return (cosine * real - sine * imag, cosine * imag + sine * real)


def full(p, like):
    return tuple(jnp.zeros_like(like) if part is None else part for part in p)


def transform(points, sign):
    count = len(points)
    if count == 1:
        return points
    if count % 2:
        sums = []
        for m in range(count):
            total = points[0]
            for s in range(1, count):
                angle = sign * 2.0 * math.pi * ((m * s) % count) / count
                term = complex_scale(points[s], math.cos(angle), math.sin(angle))
                total = complex_add(total, term)
            sums.append(total)
        return sums
    even = transform(points[0::2], sign)
    odd = transform(points[1::2], sign)
    low, high = [], []
    for m in range(count // 2):
        angle = sign * 2.0 * math.pi * m / count
        turned = complex_scale(odd[m], math.cos(angle), math.sin(angle))
        low.append(complex_add(even[m], turned))
        high.append(complex_sub(even[m], turned))
    return low + high


def pick(index, values):
    chosen = jnp.float32(values[-1])
    for place in range(len(values) - 1):
        chosen = jnp.where(index == place, jnp.float32(values[place]), chosen)
    return chosen


def forward_kernel(*refs):
    chunks, out = refs[:4], refs[4]
    steps, planes = chunks[0].shape[:2]
    length = 4 * steps
    ratio = ALPHA_CORNER ** (1.0 / length)
    me = lax.axis_index("tm")
    weights = []
    for m in range(4):
        block = jnp.bitwise_xor(me, m)
        grow = [ratio ** (steps * d) for d in range(4)]
        weights.append(
            (
                pick(block, grow),
                pick(block, [grow[0], -grow[1], grow[2], -grow[3]]),
                pick(block, [grow[0], 0.0, -grow[2], 0.0]),
                pick(block, [0.0, -grow[1], 0.0, grow[3]]),
            )
        )

    def column(j, carry):
        sums = [[], [], [], []]
        for s in range(steps):
            values = [chunk[s, j] for chunk in chunks]
            for kind in range(4):
                total = weights[0][kind] * values[0]
                for m in range(1, 4):
                    total = total + weights[m][kind] * values[m]
                sums[kind].append(total)

        def turned(real, imag, remainder):
            points = []
            for s in range(steps):
                angle = -2.0 * math.pi * remainder * s / length
                size = ratio**s
                point = (real[s], None if imag is None else imag[s])
                point = complex_scale(point, size * math.cos(angle), size * math.sin(angle))
                points.append(full(point, real[s]))
            return transform(points, -1.0)

        halves = length // 2
        found = {}
        for remainder, real, imag in ((0, sums[0], None), (2, sums[1], None), (1, sums[2], sums[3])):
            for m, value in enumerate(turned(real, imag, remainder)):
                slot = 4 * m + remainder
                if slot <= halves:
                    found[slot] = value
                elif remainder == 1:
                    found[length - slot] = (value[0], -value[1])
        out[0, 0, j] = found[0][0]
        out[0, 1, j] = found[halves][0]
        for slot in range(1, halves):
            out[slot, 0, j] = found[slot][0]
            out[slot, 1, j] = found[slot][1]
        return carry

    lax.fori_loop(0, planes, column, 0)


def backward_kernel(spectrum, *outs):
    steps, planes = outs[0].shape[:2]
    length = 4 * steps
    halves = length // 2
    ratio = ALPHA_CORNER ** (1.0 / length)
    me = lax.axis_index("tm")
    weights = []
    for m in range(4):
        block = jnp.bitwise_xor(me, m)
        grow = [ratio ** (-steps * d) / length for d in range(4)]
        weights.append(
            (
                pick(block, grow),
                pick(block, [grow[0], -grow[1], grow[2], -grow[3]]),
                pick(block, [2.0 * grow[0], 0.0, -2.0 * grow[2], 0.0]),
                pick(block, [0.0, -2.0 * grow[1], 0.0, 2.0 * grow[3]]),
            )
        )

    def column(j, carry):
        def value(slot):
            if slot == 0:
                return (spectrum[0, 0, j], jnp.zeros_like(spectrum[0, 0, j]))
            if slot == halves:
                return (spectrum[0, 1, j], jnp.zeros_like(spectrum[0, 1, j]))
            if slot < halves:
                return (spectrum[slot, 0, j], spectrum[slot, 1, j])
            return (spectrum[length - slot, 0, j], -spectrum[length - slot, 1, j])

        def turned(remainder):
            points = transform([value(4 * m + remainder) for m in range(steps)], 1.0)
            result = []
            for s in range(steps):
                angle = 2.0 * math.pi * remainder * s / length
                size = ratio**-s
                result.append(
                    complex_scale(points[s], size * math.cos(angle), size * math.sin(angle))
                )
            return result

        zero, two, one = turned(0), turned(2), turned(1)
        for s in range(steps):
            parts = (zero[s][0], two[s][0], one[s][0], one[s][1])
            for m in range(4):
                total = weights[m][0] * parts[0]
                for kind in range(1, 4):
                    total = total + weights[m][kind] * parts[kind]
                outs[m][s, j] = total
        return carry

    lax.fori_loop(0, planes, column, 0)


def place_kernel(*refs):
    chunks, out = refs[:4], refs[4]
    steps, planes = chunks[0].shape[:2]
    me = lax.axis_index("tm")

    def one_step(s, carry):
        for m in range(4):
            block = jnp.bitwise_xor(me, m)
            for j in range(planes):
                out[s, block * planes + j] = chunks[m][s, j]
        return carry

    lax.fori_loop(0, steps, one_step, 0, unroll=4)


def cycle_kernel(blocks, forcing, out, *scratch, tm_count, space_count, order):
    rows, lanes = forcing.shape[-2:]
    planes = forcing.shape[2]
    thickness = blocks.shape[1]
    slots = forcing.shape[0]
    length = 2 * slots
    ratio = ALPHA_CORNER ** (1.0 / length)
    me_space = lax.axis_index("space")
    slot = lax.axis_index("tm") * space_count + me_space
    angles = [2.0 * math.pi * k / length for k in range(slots)]
    first = [(1.0 - ratio * math.cos(a)) / STEP_SIZE for a in angles]
    second = [ratio * math.sin(a) / STEP_SIZE for a in angles]
    third = list(first)
    second[0] = 0.0
    third[0] = (1.0 + ratio) / STEP_SIZE
    first, second, third = (pick(slot, values) for values in (first, second, third))

    fields = [
        dict(zip(("capacity", "a", "b", "c", "u", "w", "g"), scratch[7 * l : 7 * l + 7]))
        for l in range(GRID_DEPTH)
    ]
    row = lax.broadcasted_iota(jnp.int32, (rows, lanes), 0)
    lane = lax.broadcasted_iota(jnp.int32, (rows, lanes), 1)

    for block, distance in enumerate(order):
        target = jnp.bitwise_xor(me_space, distance) * thickness
        for x in range(thickness):
            fields[0]["capacity"][target + x] = blocks[block, x]

    def loop(count, group, body):
        if count <= group:
            for p in range(count):
                body(0, p)
        else:
            assert count % group == 0

            def step(i, carry):
                base = i * group
                for p in range(group):
                    body(base, p)
                return carry

            lax.fori_loop(0, count // group, step, 0)

    def pair_sum(value, level):
        stride = 2**level
        if stride < rows:
            bit = (row // stride) % 2 == 1
            value = value + jnp.where(
                bit, pltpu.roll(value, stride, 0), pltpu.roll(value, rows - stride, 0)
            )
        bit = (lane // stride) % 2 == 1
        return value + jnp.where(
            bit, pltpu.roll(value, stride, 1), pltpu.roll(value, lanes - stride, 1)
        )

    def level_count(level):
        return fields[level]["capacity"].shape[0]

    for level in range(1, GRID_DEPTH):
        fine, coarse = fields[level - 1]["capacity"], fields[level]["capacity"]

        def shrink(base, p, fine=fine, coarse=coarse, level=level):
            pair = fine[2 * (base + p)] + fine[2 * (base + p) + 1]
            coarse[base + p] = 0.125 * pair_sum(pair, level - 1)

        loop(level_count(level), 8, shrink)

    def stencil(level):
        spread, drifts = level_coefficients(level)
        stride = 2**level
        extents = (rows // stride, lanes // stride)
        cell = (row // stride, lane // stride)
        masks = []
        for d in range(2):
            up = jnp.where(cell[d] < extents[d] - 1, spread - drifts[d + 1], 0.0)
            down = jnp.where(cell[d] > 0, spread + drifts[d + 1], 0.0)
            masks.append((up, down))

        def apply(here, up, down):
            total = (spread - drifts[0]) * up + (spread + drifts[0]) * down
            if extents[0] > 1:
                total = total + masks[0][0] * pltpu.roll(here, rows - stride, 0)
                total = total + masks[0][1] * pltpu.roll(here, stride, 0)
            total = total + masks[1][0] * pltpu.roll(here, lanes - stride, 1)
            return total + masks[1][1] * pltpu.roll(here, stride, 1)

        return apply

    def forcing_at(level, group, base, p):
        if level:
            ref = fields[level]["g"]
            return ref[base + p, 0], ref[base + p, 1]
        source, inner = base // thickness, p
        index = (inner // planes) * space_count + source
        return forcing[index, 0, inner % planes], forcing[index, 1, inner % planes]

    def start(level):
        field = fields[level]
        spread, _ = level_coefficients(level)
        zero = jnp.zeros((rows, lanes), jnp.float32)
        for name in ("u", "w"):
            for edge in (0, level_count(level) + 1):
                field[name][edge, 0] = zero
                field[name][edge, 1] = zero

        def body(base, p):
            here = base + p
            size = field["capacity"][here]
            top = size * first + 6.0 * spread
            couple = size * second
            bottom = size * third + 6.0 * spread
            inverse = OMEGA / (top * bottom + couple * couple)
            a, b, c = bottom * inverse, couple * inverse, top * inverse
            field["a"][here] = a
            field["b"][here] = b
            field["c"][here] = c
            real, imag = forcing_at(level, group_of(level), base, p)
            field["u"][here + 1, 0] = a * real + b * imag
            field["u"][here + 1, 1] = c * imag - b * real

        loop(level_count(level), group_of(level), body)

    def group_of(level):
        return thickness

    def right_side(level, apply, source, base, p):
        here = base + p
        real, imag = forcing_at(level, group_of(level), base, p)
        v_real, v_imag = source[here + 1, 0], source[here + 1, 1]
        r_real = real + apply(v_real, source[here + 2, 0], source[here, 0])
        r_imag = imag + apply(v_imag, source[here + 2, 1], source[here, 1])
        return v_real, v_imag, r_real, r_imag

    def sweep(level, source, store):
        field, apply = fields[level], stencil(level)

        def body(base, p):
            here = base + p
            v_real, v_imag, r_real, r_imag = right_side(level, apply, source, base, p)
            a, b, c = field["a"][here], field["b"][here], field["c"][here]
            new_real = (1.0 - OMEGA) * v_real + (a * r_real + b * r_imag)
            new_imag = (1.0 - OMEGA) * v_imag + (c * r_imag - b * r_real)
            store(base, p, new_real, new_imag)

        loop(level_count(level), group_of(level), body)

    def storing(ref):
        def store(base, p, real, imag):
            ref[base + p + 1, 0] = real
            ref[base + p + 1, 1] = imag

        return store

    def store_out(base, p, real, imag):
        index = (p // planes) * space_count + base // thickness
        out[index, 0, p % planes] = real
        out[index, 1, p % planes] = imag

    def descend(level, source):
        field, apply = fields[level], stencil(level)
        spread, _ = level_coefficients(level)
        coarse = fields[level + 1]["g"]

        def defect(base, p):
            here = base + p
            v_real, v_imag, r_real, r_imag = right_side(level, apply, source, base, p)
            size = field["capacity"][here]
            real = r_real - 6.0 * spread * v_real - size * (first * v_real - second * v_imag)
            imag = r_imag - 6.0 * spread * v_imag - size * (second * v_real + third * v_imag)
            return real, imag

        def body(base, p):
            if p % 2:
                return
            low, high = defect(base, p), defect(base, p + 1)
            target = (base + p) // 2
            for part in range(2):
                coarse[target, part] = 0.125 * pair_sum(low[part] + high[part], level)

        loop(level_count(level), group_of(level), body)

    def cycle(level, last_store):
        field = fields[level]
        here, other = field["u"], field["w"]
        start(level)
        coarsest = level == GRID_DEPTH - 1
        for repeat in range((COARSE_SWEEPS if coarsest else SMOOTH) - 1):
            sweep(level, here, storing(other))
            here, other = other, here
        if coarsest:
            return here
        descend(level, here)
        value = cycle(level + 1, None)

        def correct(base, p, here=here):
            at = base + p
            for part in range(2):
                here[at + 1, part] = here[at + 1, part] + value[at // 2 + 1, part]

        loop(level_count(level), group_of(level), correct)
        for repeat in range(SMOOTH):
            final = repeat == SMOOTH - 1 and last_store is not None
            sweep(level, here, last_store if final else storing(other))
            here, other = other, here
        return here

    cycle(0, store_out)


def call(kernel, shapes, *operands, scratch=()):
    return pl.pallas_call(
        kernel,
        out_shape=shapes,
        in_specs=[pl.BlockSpec(memory_space=pltpu.VMEM)] * len(operands),
        out_specs=jax.tree.map(lambda s: pl.BlockSpec(memory_space=pltpu.VMEM), shapes),
        scratch_shapes=scratch,
    )(*operands)


def gather_capacity(capacity, space_count):
    blocks, strides = capacity[None], []
    order = [0]
    stride = 2
    while stride < space_count:
        strides.append(stride)
        stride *= 2
    strides.append(1)
    for stride in strides:
        pairs = [(k, k ^ stride) for k in range(space_count)]
        blocks = jnp.concatenate([blocks, lax.ppermute(blocks, "space", pairs)], axis=0)
        order = order + [place ^ stride for place in order]
    return blocks, order


def slot_program(residual, capacity):
    steps, thickness, rows, lanes = residual.shape
    tm_count, space_count = lax.axis_size("tm"), lax.axis_size("space")
    slots = tm_count * space_count
    planes = thickness // tm_count
    me = lax.axis_index("tm")
    split = residual.reshape(steps, tm_count, planes, rows, lanes)
    chunks = []
    for m in range(tm_count):
        chunks.append(
            lax.dynamic_index_in_dim(split, jnp.bitwise_xor(me, m), axis=1, keepdims=False)
        )
    swaps = [[(k, k ^ m) for k in range(tm_count)] for m in range(tm_count)]
    for m in range(1, tm_count):
        chunks[m] = lax.ppermute(chunks[m], "tm", swaps[m])
    blocks, order = gather_capacity(capacity, space_count)
    spectrum = call(
        forward_kernel,
        jax.ShapeDtypeStruct((slots, 2, planes, rows, lanes), jnp.float32),
        *chunks,
    )
    spectrum = lax.all_to_all(spectrum, ("tm", "space"), 0, 0, tiled=True)
    scratch = []
    for level in range(GRID_DEPTH):
        count = (thickness * space_count) >> level
        scratch += [pltpu.VMEM((count, rows, lanes), jnp.float32)] * 4
        scratch += [pltpu.VMEM((count + 2, 2, rows, lanes), jnp.float32)] * 2
        small = level == 0
        scratch += [pltpu.VMEM((1 if small else count, 2, rows, lanes), jnp.float32)]
    solved = call(
        functools.partial(
            cycle_kernel, tm_count=tm_count, space_count=space_count, order=tuple(order)
        ),
        jax.ShapeDtypeStruct(spectrum.shape, jnp.float32),
        blocks,
        spectrum,
        scratch=scratch,
    )
    solved = lax.all_to_all(solved, ("tm", "space"), 0, 0, tiled=True)
    chunk = jax.ShapeDtypeStruct((steps, planes, rows, lanes), jnp.float32)
    pieces = list(call(backward_kernel, (chunk,) * tm_count, solved))
    for m in range(1, tm_count):
        pieces[m] = lax.ppermute(pieces[m], "tm", swaps[m])
    return call(place_kernel, jax.ShapeDtypeStruct(residual.shape, jnp.float32), *pieces)


def on_device(residual, capacity):
    steps, thickness, rows, lanes = residual.shape
    tm_count, space_count = lax.axis_size("tm"), lax.axis_size("space")
    whole = (
        tm_count == 4
        and 2 * space_count == steps
        and space_count & (space_count - 1) == 0
        and space_count > 1
        and thickness % tm_count == 0
        and thickness % 2 == 0
    )
    if whole:
        return slot_program(residual, capacity)
    return slab_program(residual, capacity)


def solution(mesh):
    return jax.shard_map(
        on_device,
        mesh=mesh,
        in_specs=(P("tm", "space", None, None), P("space", None, None)),
        out_specs=P("tm", "space", None, None),
        check_vma=False,
    )
```

profile of v0, /device:TPU:0, one launch (start us, length us, event | category | flops | bytes accessed | tf_op | source)
XLA Modules:
  0.0 86.6 jit_solution(5455381810405523562)
XLA Ops:
  0.0 1.8 %dynamic-slice_bitcast_fusion = (f32[16,2,8,128]{3,2,1,0:T(8,128)S(1)}, f32[16,2,8,128]{3,2,1,0:T(8,128)S(1)}, f32[16,2,8,128]{3,2,1,0:T(8,128)S(1)}, f32[16,2,8,128]{3,2,1,0:T(8,128)}) fusion(f32[16,4,2,8,128]{4,3,2,1,0:T(8,128)} %bitcast.18, s32[]{:T(128)S(6)} %select_n.16, s32[]{:T(128)S(6)} %select_n.15, s32[]{:T(128)S(6)} %select_n.14, s32[]{:T(128)S(6)} %select_n.13), kind=kLoop, calls=%fused_computation.2 | loop fusion | bytes 1048592 | tf_op jit(solution)/shard_map/jit(dynamic_index_in_dim)/squeeze | solution.py:682
  1.8 3.0 %collective-permute-start.3 = (f32[16,2,8,128]{3,2,1,0:T(8,128)S(1)}, f32[16,2,8,128]{3,2,1,0:T(8,128)S(1)}, u32[]{:S(2)}, u32[]{:S(2)}) collective-permute-start(f32[16,2,8,128]{3,2,1,0:T(8,128)S(1)} %get-tuple-element.15), channel_id=1, source_target_pairs={{0,8},{8,0},{16,24},{24,16},{1,9},{9,1},{17,25},{25,17},{2,10},{10... | collective-permute-start | bytes 393224 | tf_op jit(solution)/shard_map/ppermute | solution.py:686
  4.7 1.5 %collective-permute-start.4 = (f32[16,2,8,128]{3,2,1,0:T(8,128)S(1)}, f32[16,2,8,128]{3,2,1,0:T(8,128)S(1)}, u32[]{:S(2)}, u32[]{:S(2)}) collective-permute-start(f32[16,2,8,128]{3,2,1,0:T(8,128)S(1)} %get-tuple-element.14), channel_id=1, source_target_pairs={{0,16},{8,24},{16,0},{24,8},{1,17},{9,25},{17,1},{25,9},{2,18},{10... | collective-permute-start | bytes 393224 | tf_op jit(solution)/shard_map/ppermute | solution.py:686
  6.3 2.4 %collective-permute-done.3.refs_1_ = f32[16,2,8,128]{3,2,1,0:T(8,128)S(1)} collective-permute-done((f32[16,2,8,128]{3,2,1,0:T(8,128)S(1)}, f32[16,2,8,128]{3,2,1,0:T(8,128)S(1)}, u32[]{:S(2)}, u32[]{:S(2)}) %collective-permute-start.3) | collective-permute-done | bytes 131104 | tf_op jit(solution)/shard_map/ppermute | solution.py:686
  8.6 3.9 %collective-permute-done.4.refs_2_ = f32[16,2,8,128]{3,2,1,0:T(8,128)S(1)} collective-permute-done((f32[16,2,8,128]{3,2,1,0:T(8,128)S(1)}, f32[16,2,8,128]{3,2,1,0:T(8,128)S(1)}, u32[]{:S(2)}, u32[]{:S(2)}) %collective-permute-start.4) | collective-permute-done | bytes 131104 | tf_op jit(solution)/shard_map/ppermute | solution.py:686
  12.5 0.6 copy-done.4
  13.2 2.2 %shard_map.28 = f32[32,2,2,8,128]{4,3,2,1,0:T(8,128)} custom-call(f32[16,2,8,128]{3,2,1,0:T(8,128)} %get-tuple-element.16.refs_0_, f32[16,2,8,128]{3,2,1,0:T(8,128)} %copy-done.2, f32[16,2,8,128]{3,2,1,0:T(8,128)} %copy-done.4, f32[16,2,8,128]{3,2,1,0:T(8,128)} %copy-done.6), custom_call_target="tpu_custom_call" | custom-call | tf_op jit(solution)/shard_map/pallas_call | solution.py:648
  15.4 4.9 %all-to-all-start = ((f32[32,2,2,8,128]{4,3,2,1,0:T(8,128)}), f32[32,2,2,8,128]{4,3,2,1,0:T(8,128)S(1)}, u32[]{:S(2)}, u32[]{:S(2)}) async-start(f32[32,2,2,8,128]{4,3,2,1,0:T(8,128)} %shard_map.28), calls=%async_computation | async-start | bytes 1048576 | tf_op jit(solution)/shard_map/all_to_all | solution.py:693
  20.4 1.8 %collective-permute-start = (f32[1,8,8,128]{3,2,1,0:T(8,128)S(1)}, f32[1,8,8,128]{3,2,1,0:T(8,128)S(1)}, u32[]{:S(2)}, u32[]{:S(2)}) collective-permute-start(f32[1,8,8,128]{3,2,1,0:T(8,128)S(1)} %bitcast.19), channel_id=1, source_target_pairs={{0,2},{1,3},{2,0},{3,1},{4,6},{5,7},{6,4},{7,5},{8,10},{9,11},{10,... | collective-permute-start | bytes 98312 | tf_op jit(solution)/shard_map/ppermute | solution.py:667
  22.2 8.0 %collective-permute-done = f32[1,8,8,128]{3,2,1,0:T(8,128)S(1)} collective-permute-done((f32[1,8,8,128]{3,2,1,0:T(8,128)S(1)}, f32[1,8,8,128]{3,2,1,0:T(8,128)S(1)}, u32[]{:S(2)}, u32[]{:S(2)}) %collective-permute-start) | collective-permute-done | bytes 32800 | tf_op jit(solution)/shard_map/ppermute | solution.py:667
  30.2 4.5 %collective-permute-start.1 = (f32[2,8,8,128]{3,2,1,0:T(8,128)S(1)}, f32[2,8,8,128]{3,2,1,0:T(8,128)S(1)}, u32[]{:S(2)}, u32[]{:S(2)}) collective-permute-start(f32[2,8,8,128]{3,2,1,0:T(8,128)S(1)} %pad_maximum_fusion.2), channel_id=1, source_target_pairs={{0,4},{1,5},{2,6},{3,7},{4,0},{5,1},{6,2},{7,3},{8,12},{9,13},{10,... | collective-permute-start | bytes 196616 | tf_op jit(solution)/shard_map/ppermute | solution.py:667
  34.7 3.4 %collective-permute-done.1 = f32[2,8,8,128]{3,2,1,0:T(8,128)S(1)} collective-permute-done((f32[2,8,8,128]{3,2,1,0:T(8,128)S(1)}, f32[2,8,8,128]{3,2,1,0:T(8,128)S(1)}, u32[]{:S(2)}, u32[]{:S(2)}) %collective-permute-start.1) | collective-permute-done | bytes 65568 | tf_op jit(solution)/shard_map/ppermute | solution.py:667
  38.2 1.3 %collective-permute-done.2 = f32[4,8,8,128]{3,2,1,0:T(8,128)S(1)} collective-permute-done((f32[4,8,8,128]{3,2,1,0:T(8,128)S(1)}, f32[4,8,8,128]{3,2,1,0:T(8,128)S(1)}, u32[]{:S(2)}, u32[]{:S(2)}) %collective-permute-start.2) | collective-permute-done | bytes 131104 | tf_op jit(solution)/shard_map/ppermute | solution.py:667
  39.6 0.7 pad_maximum_fusion.blocks
  40.3 0.8 copy-done
  41.1 11.3 %shard_map.29 = f32[32,2,2,8,128]{4,3,2,1,0:T(8,128)} custom-call(f32[8,8,8,128]{3,2,1,0:T(8,128)} %pad_maximum_fusion.blocks, f32[32,2,2,8,128]{4,3,2,1,0:T(8,128)} %copy-done), custom_call_target="tpu_custom_call" | custom-call | tf_op jit(solution)/shard_map/pallas_call | solution.py:648
  52.3 20.3 %all_to_all.10.spectrum = f32[32,2,2,8,128]{4,3,2,1,0:T(8,128)} all-to-all(f32[32,2,2,8,128]{4,3,2,1,0:T(8,128)} %shard_map.29), channel_id=1, replica_groups=mesh['tm'=4,'space'=8] {'tm','space'}, dimensions={0} | all-to-all | bytes 1048576 | tf_op jit(solution)/shard_map/all_to_all | solution.py:710
  72.7 2.2 %shard_map.30 = (f32[16,2,8,128]{3,2,1,0:T(8,128)}, f32[16,2,8,128]{3,2,1,0:T(8,128)}, f32[16,2,8,128]{3,2,1,0:T(8,128)}, f32[16,2,8,128]{3,2,1,0:T(8,128)}) custom-call(f32[32,2,2,8,128]{4,3,2,1,0:T(8,128)} %all_to_all.10.spectrum), custom_call_target="tpu_custom_call" | custom-call | tf_op jit(solution)/shard_map/pallas_call | solution.py:648
  74.8 1.1 %collective-permute-start.7 = (f32[16,2,8,128]{3,2,1,0:T(8,128)}, f32[16,2,8,128]{3,2,1,0:T(8,128)S(1)}, u32[]{:S(2)}, u32[]{:S(2)}) collective-permute-start(f32[16,2,8,128]{3,2,1,0:T(8,128)} %get-tuple-element.11), channel_id=1, source_target_pairs={{0,16},{8,24},{16,0},{24,8},{1,17},{9,25},{17,1},{25,9},{2,18},{10... | collective-permute-start | bytes 393224 | tf_op jit(solution)/shard_map/ppermute | solution.py:714
  75.9 2.4 %collective-permute-start.8 = (f32[16,2,8,128]{3,2,1,0:T(8,128)}, f32[16,2,8,128]{3,2,1,0:T(8,128)S(1)}, u32[]{:S(2)}, u32[]{:S(2)}) collective-permute-start(f32[16,2,8,128]{3,2,1,0:T(8,128)} %get-tuple-element.12), channel_id=1, source_target_pairs={{0,24},{8,16},{16,8},{24,0},{1,25},{9,17},{17,9},{25,1},{2,26},{10... | collective-permute-start | bytes 393224 | tf_op jit(solution)/shard_map/ppermute | solution.py:714
  78.3 3.1 %collective-permute-done.6.refs_1_ = f32[16,2,8,128]{3,2,1,0:T(8,128)S(1)} collective-permute-done((f32[16,2,8,128]{3,2,1,0:T(8,128)}, f32[16,2,8,128]{3,2,1,0:T(8,128)S(1)}, u32[]{:S(2)}, u32[]{:S(2)}) %collective-permute-start.6) | collective-permute-done | bytes 131104 | tf_op jit(solution)/shard_map/ppermute | solution.py:714
  81.4 2.5 %collective-permute-done.7.refs_2_ = f32[16,2,8,128]{3,2,1,0:T(8,128)S(1)} collective-permute-done((f32[16,2,8,128]{3,2,1,0:T(8,128)}, f32[16,2,8,128]{3,2,1,0:T(8,128)S(1)}, u32[]{:S(2)}, u32[]{:S(2)}) %collective-permute-start.7) | collective-permute-done | bytes 131104 | tf_op jit(solution)/shard_map/ppermute | solution.py:714
  83.9 0.7 copy-done.5
  84.6 1.9 %shard_map.31 = f32[16,8,8,128]{3,2,1,0:T(8,128)} custom-call(f32[16,2,8,128]{3,2,1,0:T(8,128)} %get-tuple-element.9.refs_0_, f32[16,2,8,128]{3,2,1,0:T(8,128)} %copy-done.3, f32[16,2,8,128]{3,2,1,0:T(8,128)} %copy-done.5, f32[16,2,8,128]{3,2,1,0:T(8,128)} %copy-done.7), custom_call_target="tpu_custom_call" | custom-call | tf_op jit(solution)/shard_map/pallas_call | solution.py:648
  (21 shorter events, 0.2 us)
Async XLA Ops:
  1.8 6.9 %collective-permute-start.3 = (f32[16,2,8,128]{3,2,1,0:T(8,128)S(1)}, f32[16,2,8,128]{3,2,1,0:T(8,128)S(1)}, u32[]{:S(2)}, u32[]{:S(2)}) collective-permute-start(f32[16,2,8,128]{3,2,1,0:T(8,128)S(1)} %get-tuple-element.15), channel_id=1, source_target_pairs={{0,8},{8,0},{16,24},{24,16},{1,9},{9,1},{17,25},{25,17},{2,10},{10... | collective-permute-start | bytes 393224 | tf_op jit(solution)/shard_map/ppermute | solution.py:686
  4.7 7.8 %collective-permute-start.4 = (f32[16,2,8,128]{3,2,1,0:T(8,128)S(1)}, f32[16,2,8,128]{3,2,1,0:T(8,128)S(1)}, u32[]{:S(2)}, u32[]{:S(2)}) collective-permute-start(f32[16,2,8,128]{3,2,1,0:T(8,128)S(1)} %get-tuple-element.14), channel_id=1, source_target_pairs={{0,16},{8,24},{16,0},{24,8},{1,17},{9,25},{17,1},{25,9},{2,18},{10... | collective-permute-start | bytes 393224 | tf_op jit(solution)/shard_map/ppermute | solution.py:686
  6.3 6.3 %collective-permute-start.5 = (f32[16,2,8,128]{3,2,1,0:T(8,128)S(1)}, f32[16,2,8,128]{3,2,1,0:T(8,128)S(1)}, u32[]{:S(2)}, u32[]{:S(2)}) collective-permute-start(f32[16,2,8,128]{3,2,1,0:T(8,128)S(1)} %get-tuple-element.13), channel_id=1, source_target_pairs={{0,24},{8,16},{16,8},{24,0},{1,25},{9,17},{17,9},{25,1},{2,26},{10... | collective-permute-start | bytes 393224 | tf_op jit(solution)/shard_map/ppermute | solution.py:686
  8.6 3.9 %copy-start.2 = (f32[16,2,8,128]{3,2,1,0:T(8,128)}, f32[16,2,8,128]{3,2,1,0:T(8,128)S(1)}, u32[]{:S(2)}) copy-start(f32[16,2,8,128]{3,2,1,0:T(8,128)S(1)} %collective-permute-done.3.refs_1_) | copy-start | bytes 393220
  12.5 0.6 copy-start.4
  12.5 0.7 copy-start.6
  15.4 4.9 %copy-start.1 = (f32[8,8,128]{2,1,0:T(8,128)S(1)}, f32[8,8,128]{2,1,0:T(8,128)}, u32[]{:S(2)}) copy-start(f32[8,8,128]{2,1,0:T(8,128)} %param.3) | copy-start | bytes 98308
  15.4 24.8 %all-to-all-start = ((f32[32,2,2,8,128]{4,3,2,1,0:T(8,128)}), f32[32,2,2,8,128]{4,3,2,1,0:T(8,128)S(1)}, u32[]{:S(2)}, u32[]{:S(2)}) async-start(f32[32,2,2,8,128]{4,3,2,1,0:T(8,128)} %shard_map.28), calls=%async_computation | async-start | bytes 1048576 | tf_op jit(solution)/shard_map/all_to_all | solution.py:693
  20.4 9.9 %collective-permute-start = (f32[1,8,8,128]{3,2,1,0:T(8,128)S(1)}, f32[1,8,8,128]{3,2,1,0:T(8,128)S(1)}, u32[]{:S(2)}, u32[]{:S(2)}) collective-permute-start(f32[1,8,8,128]{3,2,1,0:T(8,128)S(1)} %bitcast.19), channel_id=1, source_target_pairs={{0,2},{1,3},{2,0},{3,1},{4,6},{5,7},{6,4},{7,5},{8,10},{9,11},{10,... | collective-permute-start | bytes 98312 | tf_op jit(solution)/shard_map/ppermute | solution.py:667
  30.2 7.9 %collective-permute-start.1 = (f32[2,8,8,128]{3,2,1,0:T(8,128)S(1)}, f32[2,8,8,128]{3,2,1,0:T(8,128)S(1)}, u32[]{:S(2)}, u32[]{:S(2)}) collective-permute-start(f32[2,8,8,128]{3,2,1,0:T(8,128)S(1)} %pad_maximum_fusion.2), channel_id=1, source_target_pairs={{0,4},{1,5},{2,6},{3,7},{4,0},{5,1},{6,2},{7,3},{8,12},{9,13},{10,... | collective-permute-start | bytes 196616 | tf_op jit(solution)/shard_map/ppermute | solution.py:667
  38.1 1.4 %collective-permute-start.2 = (f32[4,8,8,128]{3,2,1,0:T(8,128)S(1)}, f32[4,8,8,128]{3,2,1,0:T(8,128)S(1)}, u32[]{:S(2)}, u32[]{:S(2)}) collective-permute-start(f32[4,8,8,128]{3,2,1,0:T(8,128)S(1)} %pad_maximum_fusion.1), channel_id=1, source_target_pairs={{0,1},{1,0},{2,3},{3,2},{4,5},{5,4},{6,7},{7,6},{8,9},{9,8},{10,11... | collective-permute-start | bytes 393224 | tf_op jit(solution)/shard_map/ppermute | solution.py:667
  40.3 0.8 copy-start
  74.8 6.6 %collective-permute-start.6 = (f32[16,2,8,128]{3,2,1,0:T(8,128)}, f32[16,2,8,128]{3,2,1,0:T(8,128)S(1)}, u32[]{:S(2)}, u32[]{:S(2)}) collective-permute-start(f32[16,2,8,128]{3,2,1,0:T(8,128)} %get-tuple-element.10), channel_id=1, source_target_pairs={{0,8},{8,0},{16,24},{24,16},{1,9},{9,1},{17,25},{25,17},{2,10},{10... | collective-permute-start | bytes 393224 | tf_op jit(solution)/shard_map/ppermute | solution.py:714
  74.8 9.1 %collective-permute-start.7 = (f32[16,2,8,128]{3,2,1,0:T(8,128)}, f32[16,2,8,128]{3,2,1,0:T(8,128)S(1)}, u32[]{:S(2)}, u32[]{:S(2)}) collective-permute-start(f32[16,2,8,128]{3,2,1,0:T(8,128)} %get-tuple-element.11), channel_id=1, source_target_pairs={{0,16},{8,24},{16,0},{24,8},{1,17},{9,25},{17,1},{25,9},{2,18},{10... | collective-permute-start | bytes 393224 | tf_op jit(solution)/shard_map/ppermute | solution.py:714
  75.9 8.0 %collective-permute-start.8 = (f32[16,2,8,128]{3,2,1,0:T(8,128)}, f32[16,2,8,128]{3,2,1,0:T(8,128)S(1)}, u32[]{:S(2)}, u32[]{:S(2)}) collective-permute-start(f32[16,2,8,128]{3,2,1,0:T(8,128)} %get-tuple-element.12), channel_id=1, source_target_pairs={{0,24},{8,16},{16,8},{24,0},{1,25},{9,17},{17,9},{25,1},{2,26},{10... | collective-permute-start | bytes 393224 | tf_op jit(solution)/shard_map/ppermute | solution.py:714
  81.4 2.5 %copy-start.3 = (f32[16,2,8,128]{3,2,1,0:T(8,128)}, f32[16,2,8,128]{3,2,1,0:T(8,128)S(1)}, u32[]{:S(2)}) copy-start(f32[16,2,8,128]{3,2,1,0:T(8,128)S(1)} %collective-permute-done.6.refs_1_) | copy-start | bytes 393220
  83.9 0.7 copy-start.5
  83.9 0.7 copy-start.7
where the time goes:
time: 87 us; the launch traced here: 86.6 us
  waiting for transfers between devices  24.6 us (28%)
  blocking collectives  20.3 us (23%)
  starting transfers between devices  19.3 us (22%)
  Pallas kernels  17.6 us (20%)
  local copies, waits for them, and re-layouts  3.97 us (5%)
    all_to_all x1, blocking collectives, slot_program(): solved = lax.all_to_all(solved, ('tm', 'space'), 0, 0, tiled=True)  20.3 us
    pallas_call x4, Pallas kernels, call(): pl.pallas_call(kernel, out_shape=shapes, in_specs=[pl.BlockSpec(memory_sp...  17.6 us
    ppermute x3, waiting for transfers between devices, gather_capacity(): lax.ppermute(blocks, 'space', pairs)  12.7 us
    ppermute x3, starting transfers between devices, gather_capacity(): lax.ppermute(blocks, 'space', pairs)  6.42 us
    ppermute x3, waiting for transfers between devices, slot_program(): chunks[m] = lax.ppermute(chunks[m], 'tm', swaps[m])  6.25 us
    ppermute x3, waiting for transfers between devices, slot_program(): pieces[m] = lax.ppermute(pieces[m], 'tm', swaps[m])  5.61 us
    all_to_all x1, starting transfers between devices, slot_program(): spectrum = lax.all_to_all(spectrum, ('tm', 'space'), 0, 0, tiled=True)  4.91 us
    ppermute x3, starting transfers between devices, slot_program(): chunks[m] = lax.ppermute(chunks[m], 'tm', swaps[m])  4.49 us
  transfers between devices with their start and end apart: 10, of which 7 were waited for; matrix products, arithmetic and copies ran while one was open for 1% of the time, Pallas kernels for 0%

commit v1 on v0

--- a/solution.py
+++ b/solution.py
@@ -19,6 +19,8 @@
 ADVECT = (0.2, -0.15, 0.1)
 OMEGA = 0.7
 HIGHEST = lax.Precision.HIGHEST
+VMEM_LIMIT = 16 * 2**20
+GROUP = 2
 
 
 def extended(array, sides, width):
@@ -85,7 +87,7 @@
 
 
 def inverse_diagonal(current_capacity, spectral_shifts, per_level_values):
-    spread, drifts = level_coefficients(per_level_values)
+    spread, _ = level_coefficients(per_level_values)
     first_shift, second_shift, third_shift = spectral_shifts
     top_left = current_capacity * first_shift + 6.0 * spread
     coupling = current_capacity * second_shift
@@ -163,7 +165,7 @@
     inverse = inverse_diagonal(current_capacity, spectral_shifts, per_level_values)
     coarsest = per_level_values == GRID_DEPTH - 1
     current = damped_update(forcing_term, inverse)
-    for repeat in range((COARSE_SWEEPS if coarsest else SMOOTH) - 1):
+    for _ in range((COARSE_SWEEPS if coarsest else SMOOTH) - 1):
         current = current + damped_update(
             forcing_term
             - apply_operator(
@@ -187,7 +189,7 @@
         assemble_parts,
     )
     current = current + prolong_cells(coarse_solution)
-    for repeat in range(SMOOTH):
+    for _ in range(SMOOTH):
         current = current + damped_update(
             forcing_term
             - apply_operator(
@@ -212,7 +214,7 @@
     all_weights = jnp.power(ratio_step, jnp.arange(length, dtype=jnp.float32))
     alternate = 1.0 - 2.0 * (jnp.arange(length, dtype=jnp.int32) % 2).astype(jnp.float32)
     capacity_fields = [capacity]
-    for per_level_values in range(1, GRID_DEPTH):
+    for _ in range(1, GRID_DEPTH):
         capacity_fields.append(restrict_to_coarse(capacity_fields[-1]))
     halves = length // 2
     phases = phase_grid(halves, length)
@@ -419,22 +421,35 @@
     lax.fori_loop(0, planes, column, 0)
 
 
+def split_kernel(residual, *refs):
+    chunks, sems = refs[:-1], refs[-1]
+    planes = chunks[0].shape[1]
+    me = lax.axis_index("tm")
+    copies = []
+    for m, chunk in enumerate(chunks):
+        block = jnp.bitwise_xor(me, m)
+        source = residual.at[:, pl.ds(block * planes, planes)]
+        copies.append(pltpu.make_async_copy(source, chunk, sems.at[m]))
+        copies[-1].start()
+    for copy in copies:
+        copy.wait()
+
+
 def place_kernel(*refs):
-    chunks, out = refs[:4], refs[4]
-    steps, planes = chunks[0].shape[:2]
+    chunks, out, sems = refs[:-2], refs[-2], refs[-1]
+    planes = chunks[0].shape[1]
     me = lax.axis_index("tm")
-
-    def one_step(s, carry):
-        for m in range(4):
-            block = jnp.bitwise_xor(me, m)
-            for j in range(planes):
-                out[s, block * planes + j] = chunks[m][s, j]
-        return carry
-
-    lax.fori_loop(0, steps, one_step, 0, unroll=4)
-
-
-def cycle_kernel(blocks, forcing, out, *scratch, tm_count, space_count, order):
+    copies = []
+    for m, chunk in enumerate(chunks):
+        block = jnp.bitwise_xor(me, m)
+        target = out.at[:, pl.ds(block * planes, planes)]
+        copies.append(pltpu.make_async_copy(chunk, target, sems.at[m]))
+        copies[-1].start()
+    for copy in copies:
+        copy.wait()
+
+
+def cycle_kernel(blocks, forcing, out, *scratch, space_count, order):
     rows, lanes = forcing.shape[-2:]
     planes = forcing.shape[2]
     thickness = blocks.shape[1]
@@ -463,20 +478,18 @@
         for x in range(thickness):
             fields[0]["capacity"][target + x] = blocks[block, x]
 
-    def loop(count, group, body):
-        if count <= group:
-            for p in range(count):
-                body(0, p)
+    def loop(count, body):
+        group = min(count, GROUP * thickness)
+        assert count % group == 0 and (group % thickness == 0 or group == count)
+
+        def step(i):
+            for p in range(group):
+                body(lambda unit: i * (group // unit), p)
+
+        if count == group:
+            step(0)
         else:
-            assert count % group == 0
-
-            def step(i, carry):
-                base = i * group
-                for p in range(group):
-                    body(base, p)
-                return carry
-
-            lax.fori_loop(0, count // group, step, 0)
+            lax.fori_loop(0, count // group, lambda i, carry: (step(i), carry)[1], 0)
 
     def pair_sum(value, level):
         stride = 2**level
@@ -496,11 +509,12 @@
     for level in range(1, GRID_DEPTH):
         fine, coarse = fields[level - 1]["capacity"], fields[level]["capacity"]
 
-        def shrink(base, p, fine=fine, coarse=coarse, level=level):
-            pair = fine[2 * (base + p)] + fine[2 * (base + p) + 1]
-            coarse[base + p] = 0.125 * pair_sum(pair, level - 1)
-
-        loop(level_count(level), 8, shrink)
+        def shrink(at, p, fine=fine, coarse=coarse, level=level):
+            here = at(1) + p
+            pair = fine[2 * here] + fine[2 * here + 1]
+            coarse[here] = 0.125 * pair_sum(pair, level - 1)
+
+        loop(level_count(level), shrink)
 
     def stencil(level):
         spread, drifts = level_coefficients(level)
@@ -523,13 +537,17 @@
 
         return apply
 
-    def forcing_at(level, group, base, p):
+    def place(at, p):
+        inner = p % thickness
+        source = at(thickness) + p // thickness
+        return (inner // planes) * space_count + source, inner % planes
+
+    def forcing_at(level, at, p):
         if level:
             ref = fields[level]["g"]
-            return ref[base + p, 0], ref[base + p, 1]
-        source, inner = base // thickness, p
-        index = (inner // planes) * space_count + source
-        return forcing[index, 0, inner % planes], forcing[index, 1, inner % planes]
+            return ref[at(1) + p, 0], ref[at(1) + p, 1]
+        index, inner = place(at, p)
+        return forcing[index, 0, inner], forcing[index, 1, inner]
 
     def start(level):
         field = fields[level]
@@ -540,8 +558,8 @@
                 field[name][edge, 0] = zero
                 field[name][edge, 1] = zero
 
-        def body(base, p):
-            here = base + p
+        def body(at, p):
+            here = at(1) + p
             size = field["capacity"][here]
             top = size * first + 6.0 * spread
             couple = size * second
@@ -551,18 +569,15 @@
             field["a"][here] = a
             field["b"][here] = b
             field["c"][here] = c
-            real, imag = forcing_at(level, group_of(level), base, p)
+            real, imag = forcing_at(level, at, p)
             field["u"][here + 1, 0] = a * real + b * imag
             field["u"][here + 1, 1] = c * imag - b * real
 
-        loop(level_count(level), group_of(level), body)
-
-    def group_of(level):
-        return thickness
-
-    def right_side(level, apply, source, base, p):
-        here = base + p
-        real, imag = forcing_at(level, group_of(level), base, p)
+        loop(level_count(level), body)
+
+    def right_side(level, apply, source, at, p):
+        here = at(1) + p
+        real, imag = forcing_at(level, at, p)
         v_real, v_imag = source[here + 1, 0], source[here + 1, 1]
         r_real = real + apply(v_real, source[here + 2, 0], source[here, 0])
         r_imag = imag + apply(v_imag, source[here + 2, 1], source[here, 1])
@@ -571,57 +586,57 @@
     def sweep(level, source, store):
         field, apply = fields[level], stencil(level)
 
-        def body(base, p):
-            here = base + p
-            v_real, v_imag, r_real, r_imag = right_side(level, apply, source, base, p)
+        def body(at, p):
+            here = at(1) + p
+            v_real, v_imag, r_real, r_imag = right_side(level, apply, source, at, p)
             a, b, c = field["a"][here], field["b"][here], field["c"][here]
             new_real = (1.0 - OMEGA) * v_real + (a * r_real + b * r_imag)
             new_imag = (1.0 - OMEGA) * v_imag + (c * r_imag - b * r_real)
-            store(base, p, new_real, new_imag)
-
-        loop(level_count(level), group_of(level), body)
+            store(at, p, new_real, new_imag)
+
+        loop(level_count(level), body)
 
     def storing(ref):
-        def store(base, p, real, imag):
-            ref[base + p + 1, 0] = real
-            ref[base + p + 1, 1] = imag
+        def store(at, p, real, imag):
+            ref[at(1) + p + 1, 0] = real
+            ref[at(1) + p + 1, 1] = imag
 
         return store
 
-    def store_out(base, p, real, imag):
-        index = (p // planes) * space_count + base // thickness
-        out[index, 0, p % planes] = real
-        out[index, 1, p % planes] = imag
+    def store_out(at, p, real, imag):
+        index, inner = place(at, p)
+        out[index, 0, inner] = real
+        out[index, 1, inner] = imag
 
     def descend(level, source):
         field, apply = fields[level], stencil(level)
         spread, _ = level_coefficients(level)
         coarse = fields[level + 1]["g"]
 
-        def defect(base, p):
-            here = base + p
-            v_real, v_imag, r_real, r_imag = right_side(level, apply, source, base, p)
+        def defect(at, p):
+            here = at(1) + p
+            v_real, v_imag, r_real, r_imag = right_side(level, apply, source, at, p)
             size = field["capacity"][here]
             real = r_real - 6.0 * spread * v_real - size * (first * v_real - second * v_imag)
             imag = r_imag - 6.0 * spread * v_imag - size * (second * v_real + third * v_imag)
             return real, imag
 
-        def body(base, p):
+        def body(at, p):
             if p % 2:
                 return
-            low, high = defect(base, p), defect(base, p + 1)
-            target = (base + p) // 2
+            low, high = defect(at, p), defect(at, p + 1)
+            target = at(2) + p // 2
             for part in range(2):
                 coarse[target, part] = 0.125 * pair_sum(low[part] + high[part], level)
 
-        loop(level_count(level), group_of(level), body)
+        loop(level_count(level), body)
 
     def cycle(level, last_store):
         field = fields[level]
         here, other = field["u"], field["w"]
         start(level)
         coarsest = level == GRID_DEPTH - 1
-        for repeat in range((COARSE_SWEEPS if coarsest else SMOOTH) - 1):
+        for _ in range((COARSE_SWEEPS if coarsest else SMOOTH) - 1):
             sweep(level, here, storing(other))
             here, other = other, here
         if coarsest:
@@ -629,12 +644,13 @@
         descend(level, here)
         value = cycle(level + 1, None)
 
-        def correct(base, p, here=here):
-            at = base + p
+        def correct(at, p, here=here, other=other):
+            place = at(1) + p + 1
             for part in range(2):
-                here[at + 1, part] = here[at + 1, part] + value[at // 2 + 1, part]
-
-        loop(level_count(level), group_of(level), correct)
+                other[place, part] = here[place, part] + value[at(2) + p // 2 + 1, part]
+
+        loop(level_count(level), correct)
+        here, other = other, here
         for repeat in range(SMOOTH):
             final = repeat == SMOOTH - 1 and last_store is not None
             sweep(level, here, last_store if final else storing(other))
@@ -644,17 +660,19 @@
     cycle(0, store_out)
 
 
-def call(kernel, shapes, *operands, scratch=()):
+def call(kernel, shapes, *operands, scratch=(), space_in=pltpu.VMEM, space_out=pltpu.VMEM):
+    out_specs = jax.tree.map(lambda s: pl.BlockSpec(memory_space=space_out), shapes)
     return pl.pallas_call(
         kernel,
         out_shape=shapes,
-        in_specs=[pl.BlockSpec(memory_space=pltpu.VMEM)] * len(operands),
-        out_specs=jax.tree.map(lambda s: pl.BlockSpec(memory_space=pltpu.VMEM), shapes),
+        in_specs=[pl.BlockSpec(memory_space=space_in)] * len(operands),
+        out_specs=out_specs,
         scratch_shapes=scratch,
+        compiler_params=pltpu.CompilerParams(vmem_limit_bytes=VMEM_LIMIT),
     )(*operands)
 
 
-def gather_capacity(capacity, space_count):
+def gather_capacity(capacity, space_count, chunks):
     blocks, strides = capacity[None], []
     order = [0]
     stride = 2
@@ -663,34 +681,17 @@
         stride *= 2
     strides.append(1)
     for stride in strides:
+        if stride == 1:
+            chunks[1:], blocks = lax.optimization_barrier((chunks[1:], blocks))
         pairs = [(k, k ^ stride) for k in range(space_count)]
-        blocks = jnp.concatenate([blocks, lax.ppermute(blocks, "space", pairs)], axis=0)
+        others = lax.ppermute(blocks, "space", pairs)
+        blocks = jnp.concatenate([blocks, others], axis=0)
         order = order + [place ^ stride for place in order]
     return blocks, order
 
 
-def slot_program(residual, capacity):
-    steps, thickness, rows, lanes = residual.shape
-    tm_count, space_count = lax.axis_size("tm"), lax.axis_size("space")
-    slots = tm_count * space_count
-    planes = thickness // tm_count
-    me = lax.axis_index("tm")
-    split = residual.reshape(steps, tm_count, planes, rows, lanes)
-    chunks = []
-    for m in range(tm_count):
-        chunks.append(
-            lax.dynamic_index_in_dim(split, jnp.bitwise_xor(me, m), axis=1, keepdims=False)
-        )
-    swaps = [[(k, k ^ m) for k in range(tm_count)] for m in range(tm_count)]
-    for m in range(1, tm_count):
-        chunks[m] = lax.ppermute(chunks[m], "tm", swaps[m])
-    blocks, order = gather_capacity(capacity, space_count)
-    spectrum = call(
-        forward_kernel,
-        jax.ShapeDtypeStruct((slots, 2, planes, rows, lanes), jnp.float32),
-        *chunks,
-    )
-    spectrum = lax.all_to_all(spectrum, ("tm", "space"), 0, 0, tiled=True)
+def run_cycle(blocks, spectrum, order):
+    space_count, thickness, rows, lanes = blocks.shape
     scratch = []
     for level in range(GRID_DEPTH):
         count = (thickness * space_count) >> level
@@ -698,25 +699,54 @@
         scratch += [pltpu.VMEM((count + 2, 2, rows, lanes), jnp.float32)] * 2
         small = level == 0
         scratch += [pltpu.VMEM((1 if small else count, 2, rows, lanes), jnp.float32)]
-    solved = call(
+    return call(
         functools.partial(
-            cycle_kernel, tm_count=tm_count, space_count=space_count, order=tuple(order)
+            cycle_kernel, space_count=space_count, order=order
         ),
         jax.ShapeDtypeStruct(spectrum.shape, jnp.float32),
         blocks,
         spectrum,
         scratch=scratch,
     )
+
+
+def slot_program(residual, capacity):
+    steps, thickness, rows, lanes = residual.shape
+    tm_count, space_count = lax.axis_size("tm"), lax.axis_size("space")
+    slots = tm_count * space_count
+    planes = thickness // tm_count
+    chunk = jax.ShapeDtypeStruct((steps, planes, rows, lanes), jnp.float32)
+    sems = [pltpu.SemaphoreType.DMA((tm_count,))]
+    chunks = list(
+        call(
+            split_kernel,
+            (chunk,) * tm_count,
+            pltpu.with_memory_space_constraint(residual, pltpu.HBM),
+            scratch=sems,
+            space_in=pl.ANY,
+        )
+    )
+    swaps = [[(k, k ^ m) for k in range(tm_count)] for m in range(tm_count)]
+    for m in range(1, tm_count):
+        chunks[m] = lax.ppermute(chunks[m], "tm", swaps[m])
+    blocks, order = gather_capacity(capacity, space_count, chunks)
+    spectrum = call(
+        forward_kernel,
+        pltpu.VMEM((slots, 2, planes, rows, lanes), jnp.float32),
+        *chunks,
+    )
+    spectrum = lax.all_to_all(spectrum, ("tm", "space"), 0, 0, tiled=True)
+    solved = run_cycle(blocks, spectrum, tuple(order))
     solved = lax.all_to_all(solved, ("tm", "space"), 0, 0, tiled=True)
-    chunk = jax.ShapeDtypeStruct((steps, planes, rows, lanes), jnp.float32)
     pieces = list(call(backward_kernel, (chunk,) * tm_count, solved))
     for m in range(1, tm_count):
         pieces[m] = lax.ppermute(pieces[m], "tm", swaps[m])
-    return call(place_kernel, jax.ShapeDtypeStruct(residual.shape, jnp.float32), *pieces)
+    whole = jax.ShapeDtypeStruct(residual.shape, jnp.float32)
+    return call(place_kernel, whole, *pieces, scratch=sems, space_out=pl.ANY)
 
 
 def on_device(residual, capacity):
-    steps, thickness, rows, lanes = residual.shape
+    steps, thickness, _, _ = residual.shape
     tm_count, space_count = lax.axis_size("tm"), lax.axis_size("space")
     whole = (
         tm_count == 4

time: 87 us -> 73.4 us (0.84)
  Pallas kernels: 17.6 us -> 9.09 us
  waiting for transfers between devices: 24.6 us -> 28.9 us
  local copies, waits for them, and re-layouts: 3.97 us -> 0.01 us
  starting transfers between devices: 19.3 us -> 16 us
  blocking collectives: 20.3 us -> 18.2 us
    all_to_all x1, waiting for transfers between devices: 0.01 us -> 14.8 us  [slot_program(): spectrum = lax.all_to_all(spectrum, ('tm', 'space'), 0, 0, tiled=True)]
    ppermute x3, waiting for transfers between devices: 12.7 us -> 3.34 us  [gather_capacity(): others = lax.ppermute(blocks, 'space', pairs)]
    pallas_call x4 -> x5, Pallas kernels: 17.6 us -> 9.09 us  [call(): pl.pallas_call(kernel, out_shape=shapes, in_specs=[pl.BlockSpec(memory_sp...]
    all_to_all x1, starting transfers between devices: 4.91 us -> 2.61 us  [slot_program(): spectrum = lax.all_to_all(spectrum, ('tm', 'space'), 0, 0, tiled=True)]
    unnamed x16 -> x2, local copies, waits for them, and re-layouts: 2.19 us -> 0.01 us
    all_to_all x1, blocking collectives: 20.3 us -> 18.2 us  [slot_program(): solved = lax.all_to_all(solved, ('tm', 'space'), 0, 0, tiled=True)]
    squeeze x1 -> x0, local copies, waits for them, and re-layouts: 1.78 us -> none  [slot_program(): lax.dynamic_index_in_dim(split, jnp.bitwise_xor(me, m), axis=1, keepdims=...]
    ppermute x3, starting transfers between devices: 4.49 us -> 3.55 us  [slot_program(): chunks[m] = lax.ppermute(chunks[m], 'tm', swaps[m])]
  transfers between devices with their start and end apart: 10 -> 10, of which waited for: 7 -> 8; matrix products, arithmetic and copies ran while one was open for 1% -> 0% of each run, Pallas kernels for 0% -> 2%
where the time goes in v1:
time: 73.4 us; the launch traced here: 73.1 us
  waiting for transfers between devices  28.9 us (39%)
  blocking collectives  18.2 us (25%)
  starting transfers between devices  16 us (22%)
  Pallas kernels  9.09 us (12%)
  other arithmetic  0.79 us (1%)
    all_to_all x1, blocking collectives, slot_program(): solved = lax.all_to_all(solved, ('tm', 'space'), 0, 0, tiled=True)  18.2 us
    all_to_all x1, waiting for transfers between devices, slot_program(): spectrum = lax.all_to_all(spectrum, ('tm', 'space'), 0, 0, tiled=True)  14.8 us
    pallas_call x5, Pallas kernels, call(): pl.pallas_call(kernel, out_shape=shapes, in_specs=[pl.BlockSpec(memory_sp...  9.09 us
    ppermute x3, starting transfers between devices, gather_capacity(): others = lax.ppermute(blocks, 'space', pairs)  6.27 us
    ppermute x3, waiting for transfers between devices, slot_program(): pieces[m] = lax.ppermute(pieces[m], 'tm', swaps[m])  5.4 us
    ppermute x3, waiting for transfers between devices, slot_program(): chunks[m] = lax.ppermute(chunks[m], 'tm', swaps[m])  5.37 us
    ppermute x3, starting transfers between devices, slot_program(): chunks[m] = lax.ppermute(chunks[m], 'tm', swaps[m])  3.55 us
    ppermute x3, starting transfers between devices, slot_program(): pieces[m] = lax.ppermute(pieces[m], 'tm', swaps[m])  3.55 us
  transfers between devices with their start and end apart: 10, of which 8 were waited for; matrix products, arithmetic and copies ran while one was open for 0% of the time, Pallas kernels for 2%

profile of v1, /device:TPU:0, one launch (start us, length us, event | category | flops | bytes accessed | tf_op | source)
XLA Modules:
  0.0 73.1 jit_solution(6380163576299477840)
XLA Ops:
  0.0 3.1 %collective-permute-start.3 = (f32[1,8,8,128]{3,2,1,0:T(8,128)}, f32[1,8,8,128]{3,2,1,0:T(8,128)S(1)}, u32[]{:S(2)}, u32[]{:S(2)}) collective-permute-start(f32[1,8,8,128]{3,2,1,0:T(8,128)} %bitcast.1), channel_id=1, source_target_pairs={{0,2},{1,3},{2,0},{3,1},{4,6},{5,7},{6,4},{7,5},{8,10},{9,11},{10,... | collective-permute-start | bytes 98312 | tf_op jit(solution)/shard_map/ppermute | solution.py:687
  3.1 2.1 %collective-permute-done.3 = f32[1,8,8,128]{3,2,1,0:T(8,128)S(1)} collective-permute-done((f32[1,8,8,128]{3,2,1,0:T(8,128)}, f32[1,8,8,128]{3,2,1,0:T(8,128)S(1)}, u32[]{:S(2)}, u32[]{:S(2)}) %collective-permute-start.3) | collective-permute-done | bytes 32800 | tf_op jit(solution)/shard_map/ppermute | solution.py:687
  5.2 0.8 %pad_maximum_fusion.2 = f32[2,8,8,128]{3,2,1,0:T(8,128)S(1)} fusion(f32[1,8,8,128]{3,2,1,0:T(8,128)S(1)} %collective-permute-done.3, f32[1,8,8,128]{3,2,1,0:T(8,128)} %bitcast.2), kind=kLoop, calls=%fused_computation.2 | loop fusion | flops 16384 | bytes 131072 | tf_op jit(solution)/shard_map/concatenate | solution.py:688
  5.9 3.0 %collective-permute-start.4 = (f32[2,8,8,128]{3,2,1,0:T(8,128)S(1)}, f32[2,8,8,128]{3,2,1,0:T(8,128)S(1)}, u32[]{:S(2)}, u32[]{:S(2)}) collective-permute-start(f32[2,8,8,128]{3,2,1,0:T(8,128)S(1)} %pad_maximum_fusion.2), channel_id=1, source_target_pairs={{0,4},{1,5},{2,6},{3,7},{4,0},{5,1},{6,2},{7,3},{8,12},{9,13},{10,... | collective-permute-start | bytes 196616 | tf_op jit(solution)/shard_map/ppermute | solution.py:687
  9.0 1.1 %shard_map.28 = (f32[16,2,8,128]{3,2,1,0:T(8,128)S(1)}, f32[16,2,8,128]{3,2,1,0:T(8,128)S(1)}, f32[16,2,8,128]{3,2,1,0:T(8,128)S(1)}, f32[16,2,8,128]{3,2,1,0:T(8,128)S(1)}) custom-call(f32[16,8,8,128]{3,2,1,0:T(8,128)} %residual.1), custom_call_target="tpu_custom_call" | custom-call | tf_op jit(solution)/shard_map/pallas_call | solution.py:665
  10.1 1.6 %collective-permute-start = (f32[16,2,8,128]{3,2,1,0:T(8,128)S(1)}, f32[16,2,8,128]{3,2,1,0:T(8,128)S(1)}, u32[]{:S(2)}, u32[]{:S(2)}) collective-permute-start(f32[16,2,8,128]{3,2,1,0:T(8,128)S(1)} %get-tuple-element.17), channel_id=1, source_target_pairs={{0,8},{8,0},{16,24},{24,16},{1,9},{9,1},{17,25},{25,17},{2,10},{10... | collective-permute-start | bytes 393224 | tf_op jit(solution)/shard_map/ppermute | solution.py:731
  11.7 1.5 %collective-permute-start.1 = (f32[16,2,8,128]{3,2,1,0:T(8,128)S(1)}, f32[16,2,8,128]{3,2,1,0:T(8,128)S(1)}, u32[]{:S(2)}, u32[]{:S(2)}) collective-permute-start(f32[16,2,8,128]{3,2,1,0:T(8,128)S(1)} %get-tuple-element.18), channel_id=1, source_target_pairs={{0,16},{8,24},{16,0},{24,8},{1,17},{9,25},{17,1},{25,9},{2,18},{10... | collective-permute-start | bytes 393224 | tf_op jit(solution)/shard_map/ppermute | solution.py:731
  13.2 0.5 collective-permute-start.2
  13.7 2.7 %collective-permute-done.refs_1_ = f32[16,2,8,128]{3,2,1,0:T(8,128)S(1)} collective-permute-done((f32[16,2,8,128]{3,2,1,0:T(8,128)S(1)}, f32[16,2,8,128]{3,2,1,0:T(8,128)S(1)}, u32[]{:S(2)}, u32[]{:S(2)}) %collective-permute-start) | collective-permute-done | bytes 131104 | tf_op jit(solution)/shard_map/ppermute | solution.py:731
  16.4 1.2 %collective-permute-done.1.refs_2_ = f32[16,2,8,128]{3,2,1,0:T(8,128)S(1)} collective-permute-done((f32[16,2,8,128]{3,2,1,0:T(8,128)S(1)}, f32[16,2,8,128]{3,2,1,0:T(8,128)S(1)}, u32[]{:S(2)}, u32[]{:S(2)}) %collective-permute-start.1) | collective-permute-done | bytes 131104 | tf_op jit(solution)/shard_map/ppermute | solution.py:731
  17.6 1.5 %collective-permute-done.2.refs_3_ = f32[16,2,8,128]{3,2,1,0:T(8,128)S(1)} collective-permute-done((f32[16,2,8,128]{3,2,1,0:T(8,128)S(1)}, f32[16,2,8,128]{3,2,1,0:T(8,128)S(1)}, u32[]{:S(2)}, u32[]{:S(2)}) %collective-permute-start.2) | collective-permute-done | bytes 131104 | tf_op jit(solution)/shard_map/ppermute | solution.py:731
  19.0 1.1 %shard_map.29 = f32[32,2,2,8,128]{4,3,2,1,0:T(8,128)} custom-call(f32[16,2,8,128]{3,2,1,0:T(8,128)S(1)} %get-tuple-element.21.refs_0_, f32[16,2,8,128]{3,2,1,0:T(8,128)S(1)} %collective-permute-done.refs_1_, f32[16,2,8,128]{3,2,1,0:T(8,128)S(1)} %collective-permute-done.1.refs_2_, f32[16,2,8,128]{3,2,1,0:T(8,128)S(1)} %collective-permute-done.2.refs_3_), custom_call_target="tpu_custom_call" | custom-call | tf_op jit(solution)/shard_map/pallas_call | solution.py:665
  20.2 2.6 %all-to-all-start = ((f32[32,2,2,8,128]{4,3,2,1,0:T(8,128)}), f32[32,2,2,8,128]{4,3,2,1,0:T(8,128)S(1)}, u32[]{:S(2)}, u32[]{:S(2)}) async-start(f32[32,2,2,8,128]{4,3,2,1,0:T(8,128)} %shard_map.29), calls=%async_computation | async-start | bytes 1048576 | tf_op jit(solution)/shard_map/all_to_all | solution.py:738
  22.8 0.2 collective-permute-start.5
  22.9 1.2 %collective-permute-done.5 = f32[4,8,8,128]{3,2,1,0:T(8,128)S(1)} collective-permute-done((f32[4,8,8,128]{3,2,1,0:T(8,128)S(1)}, f32[4,8,8,128]{3,2,1,0:T(8,128)S(1)}, u32[]{:S(2)}, u32[]{:S(2)}) %collective-permute-start.5) | collective-permute-done | bytes 131104 | tf_op jit(solution)/shard_map/ppermute | solution.py:687
  24.2 14.8 %all-to-all-done.forcing = f32[32,2,2,8,128]{4,3,2,1,0:T(8,128)S(1)} async-done(((f32[32,2,2,8,128]{4,3,2,1,0:T(8,128)}), f32[32,2,2,8,128]{4,3,2,1,0:T(8,128)S(1)}, u32[]{:S(2)}, u32[]{:S(2)}) %all-to-all-start) | async-done | bytes 524320 | tf_op jit(solution)/shard_map/all_to_all | solution.py:738
  39.0 5.7 %shard_map.30 = f32[32,2,2,8,128]{4,3,2,1,0:T(8,128)S(1)} custom-call(f32[8,8,8,128]{3,2,1,0:T(8,128)S(1)} %pad_maximum_fusion.blocks, f32[32,2,2,8,128]{4,3,2,1,0:T(8,128)S(1)} %all-to-all-done.forcing), custom_call_target="tpu_custom_call" | custom-call | tf_op jit(solution)/shard_map/pallas_call | solution.py:665
  44.7 18.2 %all_to_all.10.spectrum = f32[32,2,2,8,128]{4,3,2,1,0:T(8,128)S(1)} all-to-all(f32[32,2,2,8,128]{4,3,2,1,0:T(8,128)S(1)} %shard_map.30), channel_id=1, replica_groups=mesh['tm'=4,'space'=8] {'tm','space'}, dimensions={0} | all-to-all | bytes 1048576 | tf_op jit(solution)/shard_map/all_to_all | solution.py:740
  63.0 0.3 shard_map.31
  63.4 1.1 %collective-permute-start.7 = (f32[16,2,8,128]{3,2,1,0:T(8,128)S(1)}, f32[16,2,8,128]{3,2,1,0:T(8,128)S(1)}, u32[]{:S(2)}, u32[]{:S(2)}) collective-permute-start(f32[16,2,8,128]{3,2,1,0:T(8,128)S(1)} %get-tuple-element.27), channel_id=1, source_target_pairs={{0,16},{8,24},{16,0},{24,8},{1,17},{9,25},{17,1},{25,9},{2,18},{10... | collective-permute-start | bytes 393224 | tf_op jit(solution)/shard_map/ppermute | solution.py:743
  64.5 2.4 %collective-permute-start.8 = (f32[16,2,8,128]{3,2,1,0:T(8,128)S(1)}, f32[16,2,8,128]{3,2,1,0:T(8,128)S(1)}, u32[]{:S(2)}, u32[]{:S(2)}) collective-permute-start(f32[16,2,8,128]{3,2,1,0:T(8,128)S(1)} %get-tuple-element.28), channel_id=1, source_target_pairs={{0,24},{8,16},{16,8},{24,0},{1,25},{9,17},{17,9},{25,1},{2,26},{10... | collective-permute-start | bytes 393224 | tf_op jit(solution)/shard_map/ppermute | solution.py:743
  66.8 2.9 %collective-permute-done.6.refs_1_ = f32[16,2,8,128]{3,2,1,0:T(8,128)S(1)} collective-permute-done((f32[16,2,8,128]{3,2,1,0:T(8,128)S(1)}, f32[16,2,8,128]{3,2,1,0:T(8,128)S(1)}, u32[]{:S(2)}, u32[]{:S(2)}) %collective-permute-start.6) | collective-permute-done | bytes 131104 | tf_op jit(solution)/shard_map/ppermute | solution.py:743
  69.7 2.5 %collective-permute-done.7.refs_2_ = f32[16,2,8,128]{3,2,1,0:T(8,128)S(1)} collective-permute-done((f32[16,2,8,128]{3,2,1,0:T(8,128)S(1)}, f32[16,2,8,128]{3,2,1,0:T(8,128)S(1)}, u32[]{:S(2)}, u32[]{:S(2)}) %collective-permute-start.7) | collective-permute-done | bytes 131104 | tf_op jit(solution)/shard_map/ppermute | solution.py:743
  72.3 0.8 %shard_map.32 = f32[16,8,8,128]{3,2,1,0:T(8,128)} custom-call(f32[16,2,8,128]{3,2,1,0:T(8,128)S(1)} %get-tuple-element.25.refs_0_, f32[16,2,8,128]{3,2,1,0:T(8,128)S(1)} %collective-permute-done.6.refs_1_, f32[16,2,8,128]{3,2,1,0:T(8,128)S(1)} %collective-permute-done.7.refs_2_, f32[16,2,8,128]{3,2,1,0:T(8,128)S(1)} %collective-permute-done.8.refs_3_), custom_call_target="tpu_custom_call" | custom-call | tf_op jit(solution)/shard_map/pallas_call | solution.py:665
  (7 shorter events, 0.1 us)
Async XLA Ops:
  0.0 5.2 %collective-permute-start.3 = (f32[1,8,8,128]{3,2,1,0:T(8,128)}, f32[1,8,8,128]{3,2,1,0:T(8,128)S(1)}, u32[]{:S(2)}, u32[]{:S(2)}) collective-permute-start(f32[1,8,8,128]{3,2,1,0:T(8,128)} %bitcast.1), channel_id=1, source_target_pairs={{0,2},{1,3},{2,0},{3,1},{4,6},{5,7},{6,4},{7,5},{8,10},{9,11},{10,... | collective-permute-start | bytes 98312 | tf_op jit(solution)/shard_map/ppermute | solution.py:687
  5.9 7.7 %copy-start = (f32[8,8,128]{2,1,0:T(8,128)S(1)}, f32[8,8,128]{2,1,0:T(8,128)}, u32[]{:S(2)}) copy-start(f32[8,8,128]{2,1,0:T(8,128)} %param.3) | copy-start | bytes 98308
  5.9 7.7 %collective-permute-start.4 = (f32[2,8,8,128]{3,2,1,0:T(8,128)S(1)}, f32[2,8,8,128]{3,2,1,0:T(8,128)S(1)}, u32[]{:S(2)}, u32[]{:S(2)}) collective-permute-start(f32[2,8,8,128]{3,2,1,0:T(8,128)S(1)} %pad_maximum_fusion.2), channel_id=1, source_target_pairs={{0,4},{1,5},{2,6},{3,7},{4,0},{5,1},{6,2},{7,3},{8,12},{9,13},{10,... | collective-permute-start | bytes 196616 | tf_op jit(solution)/shard_map/ppermute | solution.py:687
  10.1 6.3 %collective-permute-start = (f32[16,2,8,128]{3,2,1,0:T(8,128)S(1)}, f32[16,2,8,128]{3,2,1,0:T(8,128)S(1)}, u32[]{:S(2)}, u32[]{:S(2)}) collective-permute-start(f32[16,2,8,128]{3,2,1,0:T(8,128)S(1)} %get-tuple-element.17), channel_id=1, source_target_pairs={{0,8},{8,0},{16,24},{24,16},{1,9},{9,1},{17,25},{25,17},{2,10},{10... | collective-permute-start | bytes 393224 | tf_op jit(solution)/shard_map/ppermute | solution.py:731
  11.7 5.9 %collective-permute-start.1 = (f32[16,2,8,128]{3,2,1,0:T(8,128)S(1)}, f32[16,2,8,128]{3,2,1,0:T(8,128)S(1)}, u32[]{:S(2)}, u32[]{:S(2)}) collective-permute-start(f32[16,2,8,128]{3,2,1,0:T(8,128)S(1)} %get-tuple-element.18), channel_id=1, source_target_pairs={{0,16},{8,24},{16,0},{24,8},{1,17},{9,25},{17,1},{25,9},{2,18},{10... | collective-permute-start | bytes 393224 | tf_op jit(solution)/shard_map/ppermute | solution.py:731
  13.2 5.9 %collective-permute-start.2 = (f32[16,2,8,128]{3,2,1,0:T(8,128)S(1)}, f32[16,2,8,128]{3,2,1,0:T(8,128)S(1)}, u32[]{:S(2)}, u32[]{:S(2)}) collective-permute-start(f32[16,2,8,128]{3,2,1,0:T(8,128)S(1)} %get-tuple-element.19), channel_id=1, source_target_pairs={{0,24},{8,16},{16,8},{24,0},{1,25},{9,17},{17,9},{25,1},{2,26},{10... | collective-permute-start | bytes 393224 | tf_op jit(solution)/shard_map/ppermute | solution.py:731
  20.2 18.8 %all-to-all-start = ((f32[32,2,2,8,128]{4,3,2,1,0:T(8,128)}), f32[32,2,2,8,128]{4,3,2,1,0:T(8,128)S(1)}, u32[]{:S(2)}, u32[]{:S(2)}) async-start(f32[32,2,2,8,128]{4,3,2,1,0:T(8,128)} %shard_map.29), calls=%async_computation | async-start | bytes 1048576 | tf_op jit(solution)/shard_map/all_to_all | solution.py:738
  22.8 1.4 %collective-permute-start.5 = (f32[4,8,8,128]{3,2,1,0:T(8,128)S(1)}, f32[4,8,8,128]{3,2,1,0:T(8,128)S(1)}, u32[]{:S(2)}, u32[]{:S(2)}) collective-permute-start(f32[4,8,8,128]{3,2,1,0:T(8,128)S(1)} %pad_maximum_fusion.1), channel_id=1, source_target_pairs={{0,1},{1,0},{2,3},{3,2},{4,5},{5,4},{6,7},{7,6},{8,9},{9,8},{10,11... | collective-permute-start | bytes 393224 | tf_op jit(solution)/shard_map/ppermute | solution.py:687
  63.3 6.4 %collective-permute-start.6 = (f32[16,2,8,128]{3,2,1,0:T(8,128)S(1)}, f32[16,2,8,128]{3,2,1,0:T(8,128)S(1)}, u32[]{:S(2)}, u32[]{:S(2)}) collective-permute-start(f32[16,2,8,128]{3,2,1,0:T(8,128)S(1)} %get-tuple-element.26), channel_id=1, source_target_pairs={{0,8},{8,0},{16,24},{24,16},{1,9},{9,1},{17,25},{25,17},{2,10},{10... | collective-permute-start | bytes 393224 | tf_op jit(solution)/shard_map/ppermute | solution.py:743
  63.4 8.9 %collective-permute-start.7 = (f32[16,2,8,128]{3,2,1,0:T(8,128)S(1)}, f32[16,2,8,128]{3,2,1,0:T(8,128)S(1)}, u32[]{:S(2)}, u32[]{:S(2)}) collective-permute-start(f32[16,2,8,128]{3,2,1,0:T(8,128)S(1)} %get-tuple-element.27), channel_id=1, source_target_pairs={{0,16},{8,24},{16,0},{24,8},{1,17},{9,25},{17,1},{25,9},{2,18},{10... | collective-permute-start | bytes 393224 | tf_op jit(solution)/shard_map/ppermute | solution.py:743
  64.5 7.8 %collective-permute-start.8 = (f32[16,2,8,128]{3,2,1,0:T(8,128)S(1)}, f32[16,2,8,128]{3,2,1,0:T(8,128)S(1)}, u32[]{:S(2)}, u32[]{:S(2)}) collective-permute-start(f32[16,2,8,128]{3,2,1,0:T(8,128)S(1)} %get-tuple-element.28), channel_id=1, source_target_pairs={{0,24},{8,16},{16,8},{24,0},{1,25},{9,17},{17,9},{25,1},{2,26},{10... | collective-permute-start | bytes 393224 | tf_op jit(solution)/shard_map/ppermute | solution.py:743

commit v2 on v1

--- a/solution.py
+++ b/solution.py
@@ -421,12 +421,12 @@
     lax.fori_loop(0, planes, column, 0)
 
 
-def split_kernel(residual, *refs):
+def split_kernel(residual, *refs, swaps):
     chunks, sems = refs[:-1], refs[-1]
     planes = chunks[0].shape[1]
     me = lax.axis_index("tm")
     copies = []
-    for m, chunk in enumerate(chunks):
+    for m, chunk in zip(swaps, chunks):
         block = jnp.bitwise_xor(me, m)
         source = residual.at[:, pl.ds(block * planes, planes)]
         copies.append(pltpu.make_async_copy(source, chunk, sems.at[m]))
@@ -435,12 +435,12 @@
         copy.wait()
 
 
-def place_kernel(*refs):
-    chunks, out, sems = refs[:-2], refs[-2], refs[-1]
+def place_kernel(*refs, swaps):
+    chunks, out, sems = refs[: len(swaps)], refs[-2], refs[-1]
     planes = chunks[0].shape[1]
     me = lax.axis_index("tm")
     copies = []
-    for m, chunk in enumerate(chunks):
+    for m, chunk in zip(swaps, chunks):
         block = jnp.bitwise_xor(me, m)
         target = out.at[:, pl.ds(block * planes, planes)]
         copies.append(pltpu.make_async_copy(chunk, target, sems.at[m]))
@@ -449,10 +449,11 @@
         copy.wait()
 
 
-def cycle_kernel(blocks, forcing, out, *scratch, space_count, order):
+def cycle_kernel(*refs, space_count, order):
+    parts, (forcing, out), scratch = refs[: len(order)], refs[len(order) :][:2], refs[len(order) + 2 :]
     rows, lanes = forcing.shape[-2:]
     planes = forcing.shape[2]
-    thickness = blocks.shape[1]
+    thickness = parts[0].shape[1]
     slots = forcing.shape[0]
     length = 2 * slots
     ratio = ALPHA_CORNER ** (1.0 / length)
@@ -473,10 +474,11 @@
     row = lax.broadcasted_iota(jnp.int32, (rows, lanes), 0)
     lane = lax.broadcasted_iota(jnp.int32, (rows, lanes), 1)
 
-    for block, distance in enumerate(order):
-        target = jnp.bitwise_xor(me_space, distance) * thickness
-        for x in range(thickness):
-            fields[0]["capacity"][target + x] = blocks[block, x]
+    for part, distances in zip(parts, order):
+        for block, distance in enumerate(distances):
+            target = jnp.bitwise_xor(me_space, distance) * thickness
+            for x in range(thickness):
+                fields[0]["capacity"][target + x] = part[block, x]
 
     def loop(count, body):
         group = min(count, GROUP * thickness)
@@ -660,7 +662,13 @@
     cycle(0, store_out)
 
 
-def call(kernel, shapes, *operands, scratch=(), space_in=pltpu.VMEM, space_out=pltpu.VMEM):
+def arrived_kernel(array, same):
+    pass
+
+
+def call(
+    kernel, shapes, *operands, scratch=(), space_in=pltpu.VMEM, space_out=pltpu.VMEM, aliases=None
+):
     out_specs = jax.tree.map(lambda s: pl.BlockSpec(memory_space=space_out), shapes)
     return pl.pallas_call(
         kernel,
@@ -668,30 +676,13 @@
         in_specs=[pl.BlockSpec(memory_space=space_in)] * len(operands),
         out_specs=out_specs,
         scratch_shapes=scratch,
+        input_output_aliases=aliases or {},
         compiler_params=pltpu.CompilerParams(vmem_limit_bytes=VMEM_LIMIT),
     )(*operands)
 
 
-def gather_capacity(capacity, space_count, chunks):
-    blocks, strides = capacity[None], []
-    order = [0]
-    stride = 2
-    while stride < space_count:
-        strides.append(stride)
-        stride *= 2
-    strides.append(1)
-    for stride in strides:
-        if stride == 1:
-            chunks[1:], blocks = lax.optimization_barrier((chunks[1:], blocks))
-        pairs = [(k, k ^ stride) for k in range(space_count)]
-        others = lax.ppermute(blocks, "space", pairs)
-        blocks = jnp.concatenate([blocks, others], axis=0)
-        order = order + [place ^ stride for place in order]
-    return blocks, order
-
-
-def run_cycle(blocks, spectrum, order):
-    space_count, thickness, rows, lanes = blocks.shape
+def run_cycle(parts, spectrum, order, space_count):
+    thickness, rows, lanes = parts[0].shape[1:]
     scratch = []
     for level in range(GRID_DEPTH):
         count = (thickness * space_count) >> level
@@ -700,14 +691,29 @@
         small = level == 0
         scratch += [pltpu.VMEM((1 if small else count, 2, rows, lanes), jnp.float32)]
     return call(
-        functools.partial(
-            cycle_kernel, space_count=space_count, order=order
-        ),
+        functools.partial(cycle_kernel, space_count=space_count, order=order),
         jax.ShapeDtypeStruct(spectrum.shape, jnp.float32),
-        blocks,
+        *parts,
         spectrum,
         scratch=scratch,
     )
+
+
+def exchanged(array, axis, distance):
+    pairs = [(k, k ^ distance) for k in range(lax.axis_size(axis))]
+    return lax.ppermute(array, axis, pairs)
+
+
+def gather_capacity(capacity, space_count):
+    parts, order = [capacity[None]], [(0,)]
+    strides = [1 << k for k in range(1, space_count.bit_length() - 1)]
+    strides[1:1] = [1]
+    for stride in strides:
+        if len(parts) > 1:
+            parts, order = [jnp.concatenate(parts, axis=0)], [sum(order, ())]
+        parts.append(exchanged(parts[0], "space", stride))
+        order.append(tuple(place ^ stride for place in order[0]))
+    return parts, tuple(order)
 
 
 def slot_program(residual, capacity):
@@ -717,32 +723,53 @@
     planes = thickness // tm_count
     chunk = jax.ShapeDtypeStruct((steps, planes, rows, lanes), jnp.float32)
     sems = [pltpu.SemaphoreType.DMA((tm_count,))]
+    source = pltpu.with_memory_space_constraint(residual, pltpu.HBM)
     chunks = list(
         call(
-            split_kernel,
+            functools.partial(split_kernel, swaps=range(tm_count)),
             (chunk,) * tm_count,
-            pltpu.with_memory_space_constraint(residual, pltpu.HBM),
+            source,
             scratch=sems,
             space_in=pl.ANY,
         )
     )
-    swaps = [[(k, k ^ m) for k in range(tm_count)] for m in range(tm_count)]
     for m in range(1, tm_count):
-        chunks[m] = lax.ppermute(chunks[m], "tm", swaps[m])
-    blocks, order = gather_capacity(capacity, space_count, chunks)
+        chunks[m] = exchanged(chunks[m], "tm", m)
+    parts, order = gather_capacity(capacity, space_count)
     spectrum = call(
         forward_kernel,
-        pltpu.VMEM((slots, 2, planes, rows, lanes), jnp.float32),
+        jax.ShapeDtypeStruct((slots, 2, planes, rows, lanes), jnp.float32),
         *chunks,
     )
     spectrum = lax.all_to_all(spectrum, ("tm", "space"), 0, 0, tiled=True)
-    solved = run_cycle(blocks, spectrum, tuple(order))
+    spectrum = call(
+        arrived_kernel,
+        jax.ShapeDtypeStruct(spectrum.shape, jnp.float32),
+        spectrum,
+        space_in=pl.ANY,
+        space_out=pl.ANY,
+        aliases={0: 0},
+    )
+    solved = run_cycle(parts, spectrum, order, space_count)
     solved = lax.all_to_all(solved, ("tm", "space"), 0, 0, tiled=True)
     pieces = list(call(backward_kernel, (chunk,) * tm_count, solved))
     for m in range(1, tm_count):
-        pieces[m] = lax.ppermute(pieces[m], "tm", swaps[m])
+        pieces[m] = exchanged(pieces[m], "tm", m)
     whole = jax.ShapeDtypeStruct(residual.shape, jnp.float32)
-    return call(place_kernel, whole, *pieces, scratch=sems, space_out=pl.ANY)
+    result = ()
+    for swaps in ((0, 1, 2), (3,)):
+        result = call(
+            functools.partial(place_kernel, swaps=swaps),
+            whole,
+            *[pieces[m] for m in swaps],
+            *result,
+            scratch=sems,
+            space_in=pl.ANY,
+            space_out=pl.ANY,
+            aliases={len(swaps): 0} if result else None,
+        )
+        result = (result,)
+    return result[0]
 
 
 def on_device(residual, capacity):

time: 73.4 us -> 77 us (1.049)
  starting transfers between devices: 16 us -> 19.4 us
  blocking collectives: 18.2 us -> 19.9 us
  waiting for transfers between devices: 28.9 us -> 27.5 us
  other arithmetic: 0.79 us -> 0.02 us
    all_to_all x1, waiting for transfers between devices: 14.8 us -> 0.51 us  [slot_program(): spectrum = lax.all_to_all(spectrum, ('tm', 'space'), 0, 0, tiled=True)]
    ppermute x9, waiting for transfers between devices: 14.1 us -> 27 us  [exchanged(): return lax.ppermute(array, axis, pairs)]
    all_to_all x1, starting transfers between devices: 2.61 us -> 4.91 us  [slot_program(): spectrum = lax.all_to_all(spectrum, ('tm', 'space'), 0, 0, tiled=True)]
    all_to_all x1, blocking collectives: 18.2 us -> 19.9 us  [slot_program(): solved = lax.all_to_all(solved, ('tm', 'space'), 0, 0, tiled=True)]
    ppermute x9, starting transfers between devices: 13.4 us -> 14.5 us  [exchanged(): return lax.ppermute(array, axis, pairs)]
    concatenate x3 -> x2, other arithmetic: 0.79 us -> 0.02 us  [gather_capacity(): parts, order = ([jnp.concatenate(parts, axis=0)], [sum(order, ())])]
    pallas_call x5 -> x7, Pallas kernels: 9.09 us -> 9.75 us  [call(): pl.pallas_call(kernel, out_shape=shapes, in_specs=[pl.BlockSpec(memory_sp...]
  transfers between devices with their start and end apart: 10 -> 10, of which waited for: 8 -> 8; matrix products, arithmetic and copies ran while one was open for 0% -> 0% of each run, Pallas kernels for 2% -> 1%
where the time goes in v2:
time: 77 us; the launch traced here: 76.7 us
  waiting for transfers between devices  27.5 us (36%)
  blocking collectives  19.9 us (26%)
  starting transfers between devices  19.4 us (25%)
  Pallas kernels  9.75 us (13%)
    ppermute x9, waiting for transfers between devices, exchanged(): return lax.ppermute(array, axis, pairs)  27 us
    all_to_all x1, blocking collectives, slot_program(): solved = lax.all_to_all(solved, ('tm', 'space'), 0, 0, tiled=True)  19.9 us
    ppermute x9, starting transfers between devices, exchanged(): return lax.ppermute(array, axis, pairs)  14.5 us
    pallas_call x7, Pallas kernels, call(): pl.pallas_call(kernel, out_shape=shapes, in_specs=[pl.BlockSpec(memory_sp...  9.75 us
    all_to_all x1, starting transfers between devices, slot_program(): spectrum = lax.all_to_all(spectrum, ('tm', 'space'), 0, 0, tiled=True)  4.91 us
  transfers between devices with their start and end apart: 10, of which 8 were waited for; matrix products, arithmetic and copies ran while one was open for 0% of the time, Pallas kernels for 1%

profile of v2, /device:TPU:0, one launch (start us, length us, event | category | flops | bytes accessed | tf_op | source)
XLA Modules:
  0.0 76.7 jit_solution(13043939533976720813)
XLA Ops:
  0.0 1.1 %shard_map.28 = (f32[16,2,8,128]{3,2,1,0:T(8,128)S(1)}, f32[16,2,8,128]{3,2,1,0:T(8,128)S(1)}, f32[16,2,8,128]{3,2,1,0:T(8,128)S(1)}, f32[16,2,8,128]{3,2,1,0:T(8,128)S(1)}) custom-call(f32[16,8,8,128]{3,2,1,0:T(8,128)} %residual.1), custom_call_target="tpu_custom_call" | custom-call | tf_op jit(solution)/shard_map/pallas_call | solution.py:673
  1.1 3.0 %collective-permute-start.3 = (f32[16,2,8,128]{3,2,1,0:T(8,128)S(1)}, f32[16,2,8,128]{3,2,1,0:T(8,128)S(1)}, u32[]{:S(2)}, u32[]{:S(2)}) collective-permute-start(f32[16,2,8,128]{3,2,1,0:T(8,128)S(1)} %get-tuple-element.14), channel_id=1, source_target_pairs={{0,8},{8,0},{16,24},{24,16},{1,9},{9,1},{17,25},{25,17},{2,10},{10... | collective-permute-start | bytes 393224 | tf_op jit(solution)/shard_map/ppermute | solution.py:704
  4.2 1.5 %collective-permute-start.4 = (f32[16,2,8,128]{3,2,1,0:T(8,128)S(1)}, f32[16,2,8,128]{3,2,1,0:T(8,128)S(1)}, u32[]{:S(2)}, u32[]{:S(2)}) collective-permute-start(f32[16,2,8,128]{3,2,1,0:T(8,128)S(1)} %get-tuple-element.15), channel_id=1, source_target_pairs={{0,16},{8,24},{16,0},{24,8},{1,17},{9,25},{17,1},{25,9},{2,18},{10... | collective-permute-start | bytes 393224 | tf_op jit(solution)/shard_map/ppermute | solution.py:704
  5.7 0.0 collective-permute-start.5
  5.7 2.3 %collective-permute-done.3.refs_1_ = f32[16,2,8,128]{3,2,1,0:T(8,128)S(1)} collective-permute-done((f32[16,2,8,128]{3,2,1,0:T(8,128)S(1)}, f32[16,2,8,128]{3,2,1,0:T(8,128)S(1)}, u32[]{:S(2)}, u32[]{:S(2)}) %collective-permute-start.3) | collective-permute-done | bytes 131104 | tf_op jit(solution)/shard_map/ppermute | solution.py:704
  8.1 3.9 %collective-permute-done.4.refs_2_ = f32[16,2,8,128]{3,2,1,0:T(8,128)S(1)} collective-permute-done((f32[16,2,8,128]{3,2,1,0:T(8,128)S(1)}, f32[16,2,8,128]{3,2,1,0:T(8,128)S(1)}, u32[]{:S(2)}, u32[]{:S(2)}) %collective-permute-start.4) | collective-permute-done | bytes 131104 | tf_op jit(solution)/shard_map/ppermute | solution.py:704
  12.0 1.1 %shard_map.29 = f32[32,2,2,8,128]{4,3,2,1,0:T(8,128)} custom-call(f32[16,2,8,128]{3,2,1,0:T(8,128)S(1)} %get-tuple-element.13.refs_0_, f32[16,2,8,128]{3,2,1,0:T(8,128)S(1)} %collective-permute-done.3.refs_1_, f32[16,2,8,128]{3,2,1,0:T(8,128)S(1)} %collective-permute-done.4.refs_2_, f32[16,2,8,128]{3,2,1,0:T(8,128)S(1)} %collective-permute-done.5.refs_3_), custom_call_target="tpu_custom_call" | custom-call | tf_op jit(solution)/shard_map/pallas_call | solution.py:673
  13.1 4.9 %all-to-all-start = ((f32[32,2,2,8,128]{4,3,2,1,0:T(8,128)}), f32[32,2,2,8,128]{4,3,2,1,0:T(8,128)S(1)}, u32[]{:S(2)}, u32[]{:S(2)}) async-start(f32[32,2,2,8,128]{4,3,2,1,0:T(8,128)} %shard_map.29), calls=%async_computation | async-start | bytes 1048576 | tf_op jit(solution)/shard_map/all_to_all | solution.py:744
  18.0 1.8 %collective-permute-start = (f32[1,8,8,128]{3,2,1,0:T(8,128)S(1)}, f32[1,8,8,128]{3,2,1,0:T(8,128)S(1)}, u32[]{:S(2)}, u32[]{:S(2)}) collective-permute-start(f32[1,8,8,128]{3,2,1,0:T(8,128)S(1)} %bitcast.1), channel_id=1, source_target_pairs={{0,2},{1,3},{2,0},{3,1},{4,6},{5,7},{6,4},{7,5},{8,10},{9,11},{10,... | collective-permute-start | bytes 98312 | tf_op jit(solution)/shard_map/ppermute | solution.py:704
  19.8 8.0 %collective-permute-done = f32[1,8,8,128]{3,2,1,0:T(8,128)S(1)} collective-permute-done((f32[1,8,8,128]{3,2,1,0:T(8,128)S(1)}, f32[1,8,8,128]{3,2,1,0:T(8,128)S(1)}, u32[]{:S(2)}, u32[]{:S(2)}) %collective-permute-start) | collective-permute-done | bytes 32800 | tf_op jit(solution)/shard_map/ppermute | solution.py:704
  27.9 1.3 %collective-permute-done.1 = f32[2,8,8,128]{3,2,1,0:T(8,128)S(1)} collective-permute-done((f32[2,8,8,128]{3,2,1,0:T(8,128)S(1)}, f32[2,8,8,128]{3,2,1,0:T(8,128)S(1)}, u32[]{:S(2)}, u32[]{:S(2)}) %collective-permute-start.1) | collective-permute-done | bytes 65568 | tf_op jit(solution)/shard_map/ppermute | solution.py:704
  29.1 4.6 %collective-permute-start.2 = (f32[4,8,8,128]{3,2,1,0:T(8,128)S(1)}, f32[4,8,8,128]{3,2,1,0:T(8,128)S(1)}, u32[]{:S(2)}, u32[]{:S(2)}) collective-permute-start(f32[4,8,8,128]{3,2,1,0:T(8,128)S(1)} %pad_maximum_fusion.refs_0_), channel_id=1, source_target_pairs={{0,4},{1,5},{2,6},{3,7},{4,0},{5,1},{6,2},{7,3},{8,12},{9,13},{10,... | collective-permute-start | bytes 393224 | tf_op jit(solution)/shard_map/ppermute | solution.py:704
  33.7 0.5 all-to-all-done.array
  34.2 6.1 %collective-permute-done.2.refs_1_ = f32[4,8,8,128]{3,2,1,0:T(8,128)S(1)} collective-permute-done((f32[4,8,8,128]{3,2,1,0:T(8,128)S(1)}, f32[4,8,8,128]{3,2,1,0:T(8,128)S(1)}, u32[]{:S(2)}, u32[]{:S(2)}) %collective-permute-start.2) | collective-permute-done | bytes 131104 | tf_op jit(solution)/shard_map/ppermute | solution.py:704
  40.3 5.7 %shard_map.31 = f32[32,2,2,8,128]{4,3,2,1,0:T(8,128)S(1)} custom-call(f32[4,8,8,128]{3,2,1,0:T(8,128)S(1)} %pad_maximum_fusion.refs_0_, f32[4,8,8,128]{3,2,1,0:T(8,128)S(1)} %collective-permute-done.2.refs_1_, f32[32,2,2,8,128]{4,3,2,1,0:T(8,128)S(1)} %shard_map.30.refs_2_), custom_call_target="tpu_custom_call" | custom-call | tf_op jit(solution)/shard_map/pallas_call | solution.py:673
  46.0 19.9 %all_to_all.10.spectrum = f32[32,2,2,8,128]{4,3,2,1,0:T(8,128)S(1)} all-to-all(f32[32,2,2,8,128]{4,3,2,1,0:T(8,128)S(1)} %shard_map.31), channel_id=1, replica_groups=mesh['tm'=4,'space'=8] {'tm','space'}, dimensions={0} | all-to-all | bytes 1048576 | tf_op jit(solution)/shard_map/all_to_all | solution.py:754
  65.9 0.3 shard_map.32
  66.3 0.1 collective-permute-start.7
  66.3 1.1 %collective-permute-start.8 = (f32[16,2,8,128]{3,2,1,0:T(8,128)S(1)}, f32[16,2,8,128]{3,2,1,0:T(8,128)S(1)}, u32[]{:S(2)}, u32[]{:S(2)}) collective-permute-start(f32[16,2,8,128]{3,2,1,0:T(8,128)S(1)} %get-tuple-element.20), channel_id=1, source_target_pairs={{0,16},{8,24},{16,0},{24,8},{1,17},{9,25},{17,1},{25,9},{2,18},{10... | collective-permute-start | bytes 393224 | tf_op jit(solution)/shard_map/ppermute | solution.py:704
  67.4 2.4 %collective-permute-start.6 = (f32[16,2,8,128]{3,2,1,0:T(8,128)S(1)}, f32[16,2,8,128]{3,2,1,0:T(8,128)S(1)}, u32[]{:S(2)}, u32[]{:S(2)}) collective-permute-start(f32[16,2,8,128]{3,2,1,0:T(8,128)S(1)} %get-tuple-element.17), channel_id=1, source_target_pairs={{0,24},{8,16},{16,8},{24,0},{1,25},{9,17},{17,9},{25,1},{2,26},{10... | collective-permute-start | bytes 393224 | tf_op jit(solution)/shard_map/ppermute | solution.py:704
  69.8 2.9 %collective-permute-done.7.refs_1_ = f32[16,2,8,128]{3,2,1,0:T(8,128)S(1)} collective-permute-done((f32[16,2,8,128]{3,2,1,0:T(8,128)S(1)}, f32[16,2,8,128]{3,2,1,0:T(8,128)S(1)}, u32[]{:S(2)}, u32[]{:S(2)}) %collective-permute-start.7) | collective-permute-done | bytes 131104 | tf_op jit(solution)/shard_map/ppermute | solution.py:704
  72.7 2.5 %collective-permute-done.8.refs_2_ = f32[16,2,8,128]{3,2,1,0:T(8,128)S(1)} collective-permute-done((f32[16,2,8,128]{3,2,1,0:T(8,128)S(1)}, f32[16,2,8,128]{3,2,1,0:T(8,128)S(1)}, u32[]{:S(2)}, u32[]{:S(2)}) %collective-permute-start.8) | collective-permute-done | bytes 131104 | tf_op jit(solution)/shard_map/ppermute | solution.py:704
  75.2 0.8 %shard_map.33.refs_1_ = f32[16,8,8,128]{3,2,1,0:T(8,128)} custom-call(f32[16,2,8,128]{3,2,1,0:T(8,128)S(1)} %get-tuple-element.18.refs_0_, f32[16,2,8,128]{3,2,1,0:T(8,128)S(1)} %collective-permute-done.7.refs_1_, f32[16,2,8,128]{3,2,1,0:T(8,128)S(1)} %collective-permute-done.8.refs_2_), custom_call_target="tpu_custom_call" | custom-call | tf_op jit(solution)/shard_map/pallas_call | solution.py:673
  76.0 0.7 shard_map.34
  (8 shorter events, 0.0 us)
Async XLA Ops:
  1.1 6.9 %collective-permute-start.3 = (f32[16,2,8,128]{3,2,1,0:T(8,128)S(1)}, f32[16,2,8,128]{3,2,1,0:T(8,128)S(1)}, u32[]{:S(2)}, u32[]{:S(2)}) collective-permute-start(f32[16,2,8,128]{3,2,1,0:T(8,128)S(1)} %get-tuple-element.14), channel_id=1, source_target_pairs={{0,8},{8,0},{16,24},{24,16},{1,9},{9,1},{17,25},{25,17},{2,10},{10... | collective-permute-start | bytes 393224 | tf_op jit(solution)/shard_map/ppermute | solution.py:704
  4.2 7.8 %collective-permute-start.4 = (f32[16,2,8,128]{3,2,1,0:T(8,128)S(1)}, f32[16,2,8,128]{3,2,1,0:T(8,128)S(1)}, u32[]{:S(2)}, u32[]{:S(2)}) collective-permute-start(f32[16,2,8,128]{3,2,1,0:T(8,128)S(1)} %get-tuple-element.15), channel_id=1, source_target_pairs={{0,16},{8,24},{16,0},{24,8},{1,17},{9,25},{17,1},{25,9},{2,18},{10... | collective-permute-start | bytes 393224 | tf_op jit(solution)/shard_map/ppermute | solution.py:704
  5.7 6.3 %collective-permute-start.5 = (f32[16,2,8,128]{3,2,1,0:T(8,128)S(1)}, f32[16,2,8,128]{3,2,1,0:T(8,128)S(1)}, u32[]{:S(2)}, u32[]{:S(2)}) collective-permute-start(f32[16,2,8,128]{3,2,1,0:T(8,128)S(1)} %get-tuple-element.16), channel_id=1, source_target_pairs={{0,24},{8,16},{16,8},{24,0},{1,25},{9,17},{17,9},{25,1},{2,26},{10... | collective-permute-start | bytes 393224 | tf_op jit(solution)/shard_map/ppermute | solution.py:704
  13.1 4.9 %copy-start = (f32[8,8,128]{2,1,0:T(8,128)S(1)}, f32[8,8,128]{2,1,0:T(8,128)}, u32[]{:S(2)}) copy-start(f32[8,8,128]{2,1,0:T(8,128)} %param.3) | copy-start | bytes 98308
  13.1 21.2 %all-to-all-start = ((f32[32,2,2,8,128]{4,3,2,1,0:T(8,128)}), f32[32,2,2,8,128]{4,3,2,1,0:T(8,128)S(1)}, u32[]{:S(2)}, u32[]{:S(2)}) async-start(f32[32,2,2,8,128]{4,3,2,1,0:T(8,128)} %shard_map.29), calls=%async_computation | async-start | bytes 1048576 | tf_op jit(solution)/shard_map/all_to_all | solution.py:744
  18.0 9.9 %collective-permute-start = (f32[1,8,8,128]{3,2,1,0:T(8,128)S(1)}, f32[1,8,8,128]{3,2,1,0:T(8,128)S(1)}, u32[]{:S(2)}, u32[]{:S(2)}) collective-permute-start(f32[1,8,8,128]{3,2,1,0:T(8,128)S(1)} %bitcast.1), channel_id=1, source_target_pairs={{0,2},{1,3},{2,0},{3,1},{4,6},{5,7},{6,4},{7,5},{8,10},{9,11},{10,... | collective-permute-start | bytes 98312 | tf_op jit(solution)/shard_map/ppermute | solution.py:704
  27.9 1.3 %collective-permute-start.1 = (f32[2,8,8,128]{3,2,1,0:T(8,128)S(1)}, f32[2,8,8,128]{3,2,1,0:T(8,128)S(1)}, u32[]{:S(2)}, u32[]{:S(2)}) collective-permute-start(f32[2,8,8,128]{3,2,1,0:T(8,128)S(1)} %pad_maximum_fusion.1), channel_id=1, source_target_pairs={{0,1},{1,0},{2,3},{3,2},{4,5},{5,4},{6,7},{7,6},{8,9},{9,8},{10,11... | collective-permute-start | bytes 196616 | tf_op jit(solution)/shard_map/ppermute | solution.py:704
  29.1 11.2 %collective-permute-start.2 = (f32[4,8,8,128]{3,2,1,0:T(8,128)S(1)}, f32[4,8,8,128]{3,2,1,0:T(8,128)S(1)}, u32[]{:S(2)}, u32[]{:S(2)}) collective-permute-start(f32[4,8,8,128]{3,2,1,0:T(8,128)S(1)} %pad_maximum_fusion.refs_0_), channel_id=1, source_target_pairs={{0,4},{1,5},{2,6},{3,7},{4,0},{5,1},{6,2},{7,3},{8,12},{9,13},{10,... | collective-permute-start | bytes 393224 | tf_op jit(solution)/shard_map/ppermute | solution.py:704
  66.3 6.4 %collective-permute-start.7 = (f32[16,2,8,128]{3,2,1,0:T(8,128)S(1)}, f32[16,2,8,128]{3,2,1,0:T(8,128)S(1)}, u32[]{:S(2)}, u32[]{:S(2)}) collective-permute-start(f32[16,2,8,128]{3,2,1,0:T(8,128)S(1)} %get-tuple-element.19), channel_id=1, source_target_pairs={{0,8},{8,0},{16,24},{24,16},{1,9},{9,1},{17,25},{25,17},{2,10},{10... | collective-permute-start | bytes 393224 | tf_op jit(solution)/shard_map/ppermute | solution.py:704
  66.3 8.9 %collective-permute-start.8 = (f32[16,2,8,128]{3,2,1,0:T(8,128)S(1)}, f32[16,2,8,128]{3,2,1,0:T(8,128)S(1)}, u32[]{:S(2)}, u32[]{:S(2)}) collective-permute-start(f32[16,2,8,128]{3,2,1,0:T(8,128)S(1)} %get-tuple-element.20), channel_id=1, source_target_pairs={{0,16},{8,24},{16,0},{24,8},{1,17},{9,25},{17,1},{25,9},{2,18},{10... | collective-permute-start | bytes 393224 | tf_op jit(solution)/shard_map/ppermute | solution.py:704
  67.4 8.6 %collective-permute-start.6 = (f32[16,2,8,128]{3,2,1,0:T(8,128)S(1)}, f32[16,2,8,128]{3,2,1,0:T(8,128)S(1)}, u32[]{:S(2)}, u32[]{:S(2)}) collective-permute-start(f32[16,2,8,128]{3,2,1,0:T(8,128)S(1)} %get-tuple-element.17), channel_id=1, source_target_pairs={{0,24},{8,16},{16,8},{24,0},{1,25},{9,17},{17,9},{25,1},{2,26},{10... | collective-permute-start | bytes 393224 | tf_op jit(solution)/shard_map/ppermute | solution.py:704
